TPU v7x, 8 devices: a whole 2x2x1 slice. The times are simulated.
8 devices in a mesh: ens: 1 (over z), sp: 8 (over y, x, core).
Axes of the slice: x: 2, y: 2, z: 1, core: 2. Of those that a mesh axis runs over, the one named last changes fastest.
Arguments:
- x_seq: bfloat16 [8192, 256], P(('ens', 'sp'))
- w_past: bfloat16 [2, 10, 256, 512], replicated
- w_now: bfloat16 [2, 10, 256, 512], replicated
- b_conv: float32 [2, 10, 512], replicated
- w_res: bfloat16 [2, 10, 256, 256], replicated
- w_skip: bfloat16 [2, 10, 256, 256], replicated
- w_out1: bfloat16 [256, 256], replicated
- b_out1: float32 [256], replicated
- w_out2: bfloat16 [256, 256], replicated
- b_out2: float32 [256], replicated
Outputs:
- output 1: float32 [8192, 256], P(('ens', 'sp'))
- output 2: bfloat16 [8192, 256], P(('ens', 'sp'))
All inputs are finite; a program needn't handle non-finite values.
Results may differ from a plain program's by a relative error of at most 0.0159135.
Values are sent between devices in bfloat16 or wider.
A program may use at most 1 GiB of HBM per device.

v0:
```python
import jax
import jax.numpy as jnp
from jax import lax
from jax.sharding import PartitionSpec as P


def solution(mesh):
    seq_devs = mesh.shape["sp"]
    shift_perm = [(src, src + 1) for src in range(seq_devs - 1)]
    row_spec = P(("ens", "sp"), None)

    def local_stack(x_seq, w_past, w_now, b_conv, w_res, w_skip, w_out1, b_out1, w_out2, b_out2):
        stacks, cycle = w_past.shape[0], w_past.shape[1]
        gate_ch = b_conv.shape[-1] // 2
        hidden = x_seq
        skip_sum = jnp.zeros((x_seq.shape[0], w_skip.shape[-1]), jnp.float32)
        for stack_idx in range(stacks):
            for layer_pos in range(cycle):
                dilation = 2 ** layer_pos
                halo_rows = lax.ppermute(hidden[-dilation:], "sp", perm=shift_perm)
                shifted = jnp.concatenate([halo_rows, hidden[:-dilation]], axis=0)
                pre_act = (jnp.dot(shifted, w_past[stack_idx, layer_pos], preferred_element_type=jnp.float32)
                           + jnp.dot(hidden, w_now[stack_idx, layer_pos], preferred_element_type=jnp.float32)
                           + b_conv[stack_idx, layer_pos])
                gated = (jnp.tanh(pre_act[:, :gate_ch]) * jax.nn.sigmoid(pre_act[:, gate_ch:])).astype(jnp.bfloat16)
                hidden = (hidden.astype(jnp.float32) + jnp.dot(gated, w_res[stack_idx, layer_pos], preferred_element_type=jnp.float32)).astype(jnp.bfloat16)
                skip_sum = skip_sum + jnp.dot(gated, w_skip[stack_idx, layer_pos], preferred_element_type=jnp.float32)
        skip_act = jax.nn.relu(skip_sum).astype(jnp.bfloat16)
        mid_act = jax.nn.relu(jnp.dot(skip_act, w_out1, preferred_element_type=jnp.float32) + b_out1).astype(jnp.bfloat16)
        logits = jnp.dot(mid_act, w_out2, preferred_element_type=jnp.float32) + b_out2
        return (logits, hidden)

    return jax.shard_map(
        local_stack,
        mesh=mesh,
        in_specs=(row_spec, P(), P(), P(), P(), P(), P(), P(), P(), P()),
        out_specs=(row_spec, row_spec),
        check_vma=False,
    )
```

profile of v0, /device:TPU:4, one launch (start us, length us, event | category | flops | bytes accessed | tf_op | source)
XLA Modules:
  0.0 164.8 jit_solution(16905835173362321025)
XLA Ops:
  5.1 2.1 %collective-permute-done = bf16[1,256]{1,0:T(2,128)(2,1)S(1)} collective-permute-done((bf16[1,256]{1,0:T(2,128)(2,1)S(1)}, bf16[1,256]{1,0:T(2,128)(2,1)S(1)}, u32[]{:S(2)}, u32[]{:S(2)}) %collective-permute-start) | collective-permute-done | bytes 544 | tf_op jit(solution)/shard_map/ppermute | solution.py:20
  10.0 2.1 %collective-permute-start.1 = (bf16[2,256]{1,0:T(2,128)(2,1)S(1)}, bf16[2,256]{1,0:T(2,128)(2,1)S(1)}, u32[]{:S(2)}, u32[]{:S(2)}) collective-permute-start(bf16[2,256]{1,0:T(2,128)(2,1)S(1)} %slice.722), channel_id=1, source_target_pairs={{0,1},{1,2},{2,3},{3,4},{4,5},{5,6},{6,7}} | collective-permute-start | bytes 3080 | tf_op jit(solution)/shard_map/ppermute | solution.py:20
  12.4 3.4 %collective-permute-done.1 = bf16[2,256]{1,0:T(2,128)(2,1)S(1)} collective-permute-done((bf16[2,256]{1,0:T(2,128)(2,1)S(1)}, bf16[2,256]{1,0:T(2,128)(2,1)S(1)}, u32[]{:S(2)}, u32[]{:S(2)}) %collective-permute-start.1) | collective-permute-done | bytes 1056 | tf_op jit(solution)/shard_map/ppermute | solution.py:20
  17.4 1.9 %collective-permute-start.2 = (bf16[4,256]{1,0:T(4,128)(2,1)S(1)}, bf16[4,256]{1,0:T(4,128)(2,1)S(1)}, u32[]{:S(2)}, u32[]{:S(2)}) collective-permute-start(bf16[4,256]{1,0:T(4,128)(2,1)S(1)} %slice.726), channel_id=1, source_target_pairs={{0,1},{1,2},{2,3},{3,4},{4,5},{5,6},{6,7}} | collective-permute-start | bytes 6152 | tf_op jit(solution)/shard_map/ppermute | solution.py:20
  19.6 3.6 %collective-permute-done.2 = bf16[4,256]{1,0:T(4,128)(2,1)S(1)} collective-permute-done((bf16[4,256]{1,0:T(4,128)(2,1)S(1)}, bf16[4,256]{1,0:T(4,128)(2,1)S(1)}, u32[]{:S(2)}, u32[]{:S(2)}) %collective-permute-start.2) | collective-permute-done | bytes 2080 | tf_op jit(solution)/shard_map/ppermute | solution.py:20
  27.1 3.5 %collective-permute-done.3 = bf16[8,256]{1,0:T(8,128)(2,1)S(1)} collective-permute-done((bf16[8,256]{1,0:T(8,128)(2,1)S(1)}, bf16[8,256]{1,0:T(8,128)(2,1)S(1)}, u32[]{:S(2)}, u32[]{:S(2)}) %collective-permute-start.3) | collective-permute-done | bytes 4128 | tf_op jit(solution)/shard_map/ppermute | solution.py:20
  34.5 3.6 %collective-permute-done.4 = bf16[16,256]{1,0:T(8,128)(2,1)S(1)} collective-permute-done((bf16[16,256]{1,0:T(8,128)(2,1)S(1)}, bf16[16,256]{1,0:T(8,128)(2,1)S(1)}, u32[]{:S(2)}, u32[]{:S(2)}) %collective-permute-start.4) | collective-permute-done | bytes 8224 | tf_op jit(solution)/shard_map/ppermute | solution.py:20
  42.0 3.7 %collective-permute-done.5 = bf16[32,256]{1,0:T(8,128)(2,1)S(1)} collective-permute-done((bf16[32,256]{1,0:T(8,128)(2,1)S(1)}, bf16[32,256]{1,0:T(8,128)(2,1)S(1)}, u32[]{:S(2)}, u32[]{:S(2)}) %collective-permute-start.5) | collective-permute-done | bytes 16416 | tf_op jit(solution)/shard_map/ppermute | solution.py:20
  49.5 3.9 %collective-permute-done.6 = bf16[64,256]{1,0:T(8,128)(2,1)S(1)} collective-permute-done((bf16[64,256]{1,0:T(8,128)(2,1)S(1)}, bf16[64,256]{1,0:T(8,128)(2,1)S(1)}, u32[]{:S(2)}, u32[]{:S(2)}) %collective-permute-start.6) | collective-permute-done | bytes 32800 | tf_op jit(solution)/shard_map/ppermute | solution.py:20
  55.0 2.1 %collective-permute-start.7 = (bf16[128,256]{1,0:T(8,128)(2,1)S(1)}, bf16[128,256]{1,0:T(8,128)(2,1)S(1)}, u32[]{:S(2)}, u32[]{:S(2)}) collective-permute-start(bf16[128,256]{1,0:T(8,128)(2,1)S(1)} %slice.746), channel_id=1, source_target_pairs={{0,1},{1,2},{2,3},{3,4},{4,5},{5,6},{6,7}} | collective-permute-start | bytes 196616 | tf_op jit(solution)/shard_map/ppermute | solution.py:20
  57.5 4.0 %collective-permute-done.7 = bf16[128,256]{1,0:T(8,128)(2,1)S(1)} collective-permute-done((bf16[128,256]{1,0:T(8,128)(2,1)S(1)}, bf16[128,256]{1,0:T(8,128)(2,1)S(1)}, u32[]{:S(2)}, u32[]{:S(2)}) %collective-permute-start.7) | collective-permute-done | bytes 65568 | tf_op jit(solution)/shard_map/ppermute | solution.py:20
  65.4 4.9 %collective-permute-done.8 = bf16[256,256]{1,0:T(8,128)(2,1)S(1)} collective-permute-done((bf16[256,256]{1,0:T(8,128)(2,1)S(1)}, bf16[256,256]{1,0:T(8,128)(2,1)S(1)}, u32[]{:S(2)}, u32[]{:S(2)}) %collective-permute-start.8) | collective-permute-done | bytes 131104 | tf_op jit(solution)/shard_map/ppermute | solution.py:20
  74.2 6.4 %collective-permute-done.9 = bf16[512,256]{1,0:T(8,128)(2,1)S(1)} collective-permute-done((bf16[512,256]{1,0:T(8,128)(2,1)S(1)}, bf16[512,256]{1,0:T(8,128)(2,1)S(1)}, u32[]{:S(2)}, u32[]{:S(2)}) %collective-permute-start.9) | collective-permute-done | bytes 262176 | tf_op jit(solution)/shard_map/ppermute | solution.py:20
  84.4 3.6 %collective-permute-done.10 = bf16[1,256]{1,0:T(2,128)(2,1)S(1)} collective-permute-done((bf16[1,256]{1,0:T(2,128)(2,1)S(1)}, bf16[1,256]{1,0:T(2,128)(2,1)S(1)}, u32[]{:S(2)}, u32[]{:S(2)}) %collective-permute-start.10) | collective-permute-done | bytes 544 | tf_op jit(solution)/shard_map/ppermute | solution.py:20
  91.8 3.6 %collective-permute-done.11 = bf16[2,256]{1,0:T(2,128)(2,1)S(1)} collective-permute-done((bf16[2,256]{1,0:T(2,128)(2,1)S(1)}, bf16[2,256]{1,0:T(2,128)(2,1)S(1)}, u32[]{:S(2)}, u32[]{:S(2)}) %collective-permute-start.11) | collective-permute-done | bytes 1056 | tf_op jit(solution)/shard_map/ppermute | solution.py:20
  99.2 3.6 %collective-permute-done.12 = bf16[4,256]{1,0:T(4,128)(2,1)S(1)} collective-permute-done((bf16[4,256]{1,0:T(4,128)(2,1)S(1)}, bf16[4,256]{1,0:T(4,128)(2,1)S(1)}, u32[]{:S(2)}, u32[]{:S(2)}) %collective-permute-start.12) | collective-permute-done | bytes 2080 | tf_op jit(solution)/shard_map/ppermute | solution.py:20
  106.6 3.5 %collective-permute-done.13 = bf16[8,256]{1,0:T(8,128)(2,1)S(1)} collective-permute-done((bf16[8,256]{1,0:T(8,128)(2,1)S(1)}, bf16[8,256]{1,0:T(8,128)(2,1)S(1)}, u32[]{:S(2)}, u32[]{:S(2)}) %collective-permute-start.13) | collective-permute-done | bytes 4128 | tf_op jit(solution)/shard_map/ppermute | solution.py:20
  111.8 2.1 %collective-permute-start.14 = (bf16[16,256]{1,0:T(8,128)(2,1)S(1)}, bf16[16,256]{1,0:T(8,128)(2,1)S(1)}, u32[]{:S(2)}, u32[]{:S(2)}) collective-permute-start(bf16[16,256]{1,0:T(8,128)(2,1)S(1)} %slice.774), channel_id=1, source_target_pairs={{0,1},{1,2},{2,3},{3,4},{4,5},{5,6},{6,7}} | collective-permute-start | bytes 24584 | tf_op jit(solution)/shard_map/ppermute | solution.py:20
  114.3 3.4 %collective-permute-done.14 = bf16[16,256]{1,0:T(8,128)(2,1)S(1)} collective-permute-done((bf16[16,256]{1,0:T(8,128)(2,1)S(1)}, bf16[16,256]{1,0:T(8,128)(2,1)S(1)}, u32[]{:S(2)}, u32[]{:S(2)}) %collective-permute-start.14) | collective-permute-done | bytes 8224 | tf_op jit(solution)/shard_map/ppermute | solution.py:20
  121.5 3.7 %collective-permute-done.15 = bf16[32,256]{1,0:T(8,128)(2,1)S(1)} collective-permute-done((bf16[32,256]{1,0:T(8,128)(2,1)S(1)}, bf16[32,256]{1,0:T(8,128)(2,1)S(1)}, u32[]{:S(2)}, u32[]{:S(2)}) %collective-permute-start.15) | collective-permute-done | bytes 16416 | tf_op jit(solution)/shard_map/ppermute | solution.py:20
  129.1 3.9 %collective-permute-done.16 = bf16[64,256]{1,0:T(8,128)(2,1)S(1)} collective-permute-done((bf16[64,256]{1,0:T(8,128)(2,1)S(1)}, bf16[64,256]{1,0:T(8,128)(2,1)S(1)}, u32[]{:S(2)}, u32[]{:S(2)}) %collective-permute-start.16) | collective-permute-done | bytes 32800 | tf_op jit(solution)/shard_map/ppermute | solution.py:20
  136.8 4.2 %collective-permute-done.17 = bf16[128,256]{1,0:T(8,128)(2,1)S(1)} collective-permute-done((bf16[128,256]{1,0:T(8,128)(2,1)S(1)}, bf16[128,256]{1,0:T(8,128)(2,1)S(1)}, u32[]{:S(2)}, u32[]{:S(2)}) %collective-permute-start.17) | collective-permute-done | bytes 65568 | tf_op jit(solution)/shard_map/ppermute | solution.py:20
  144.9 4.9 %collective-permute-done.18 = bf16[256,256]{1,0:T(8,128)(2,1)S(1)} collective-permute-done((bf16[256,256]{1,0:T(8,128)(2,1)S(1)}, bf16[256,256]{1,0:T(8,128)(2,1)S(1)}, u32[]{:S(2)}, u32[]{:S(2)}) %collective-permute-start.18) | collective-permute-done | bytes 131104 | tf_op jit(solution)/shard_map/ppermute | solution.py:20
  153.7 6.4 %collective-permute-done.19 = bf16[512,256]{1,0:T(8,128)(2,1)S(1)} collective-permute-done((bf16[512,256]{1,0:T(8,128)(2,1)S(1)}, bf16[512,256]{1,0:T(8,128)(2,1)S(1)}, u32[]{:S(2)}, u32[]{:S(2)}) %collective-permute-start.19) | collective-permute-done | bytes 262176 | tf_op jit(solution)/shard_map/ppermute | solution.py:20
  (174 shorter events, 75.1 us)
Async XLA Ops:
  0.6 161.4 %copy-start = (bf16[256,256]{1,0:T(8,128)(2,1)S(1)}, bf16[256,256]{1,0:T(8,128)(2,1)}, u32[]{:S(2)}) copy-start(bf16[256,256]{1,0:T(8,128)(2,1)} %param.16) | copy-start | bytes 393220
  1.4 5.8 %collective-permute-start = (bf16[1,256]{1,0:T(2,128)(2,1)S(1)}, bf16[1,256]{1,0:T(2,128)(2,1)S(1)}, u32[]{:S(2)}, u32[]{:S(2)}) collective-permute-start(bf16[1,256]{1,0:T(2,128)(2,1)S(1)} %slice.540), channel_id=1, source_target_pairs={{0,1},{1,2},{2,3},{3,4},{4,5},{5,6},{6,7}} | collective-permute-start | bytes 1544 | tf_op jit(solution)/shard_map/ppermute | solution.py:20
  3.4 8.7 %copy-start.4 = (bf16[2,10,256,256]{3,2,1,0:T(8,128)(2,1)S(1)}, bf16[2,10,256,256]{3,2,1,0:T(8,128)(2,1)}, u32[]{:S(2)}) copy-start(bf16[2,10,256,256]{3,2,1,0:T(8,128)(2,1)} %param.15) | copy-start | bytes 7864324
  7.2 8.5 %slice-start = ((s8[5242880]{0:T(1024)(128)(4,1)}), s8[4194304]{0:T(1024)(128)(4,1)S(1)}, s32[]{:S(2)}) async-start(s8[5242880]{0:T(1024)(128)(4,1)} %bitcast.335), calls=%async_computation | async-start | bytes 8388608
  8.8 7.0 %slice-start.1 = ((s8[5242880]{0:T(1024)(128)(4,1)}), s8[1048576]{0:T(1024)(128)(4,1)S(1)}, s32[]{:S(2)}) async-start(s8[5242880]{0:T(1024)(128)(4,1)} %bitcast.335), calls=%async_computation.1 | async-start | bytes 2097152
  10.0 5.8 %collective-permute-start.1 = (bf16[2,256]{1,0:T(2,128)(2,1)S(1)}, bf16[2,256]{1,0:T(2,128)(2,1)S(1)}, u32[]{:S(2)}, u32[]{:S(2)}) collective-permute-start(bf16[2,256]{1,0:T(2,128)(2,1)S(1)} %slice.722), channel_id=1, source_target_pairs={{0,1},{1,2},{2,3},{3,4},{4,5},{5,6},{6,7}} | collective-permute-start | bytes 3080 | tf_op jit(solution)/shard_map/ppermute | solution.py:20
  17.4 5.8 %collective-permute-start.2 = (bf16[4,256]{1,0:T(4,128)(2,1)S(1)}, bf16[4,256]{1,0:T(4,128)(2,1)S(1)}, u32[]{:S(2)}, u32[]{:S(2)}) collective-permute-start(bf16[4,256]{1,0:T(4,128)(2,1)S(1)} %slice.726), channel_id=1, source_target_pairs={{0,1},{1,2},{2,3},{3,4},{4,5},{5,6},{6,7}} | collective-permute-start | bytes 6152 | tf_op jit(solution)/shard_map/ppermute | solution.py:20
  24.8 5.8 %collective-permute-start.3 = (bf16[8,256]{1,0:T(8,128)(2,1)S(1)}, bf16[8,256]{1,0:T(8,128)(2,1)S(1)}, u32[]{:S(2)}, u32[]{:S(2)}) collective-permute-start(bf16[8,256]{1,0:T(8,128)(2,1)S(1)} %slice.730), channel_id=1, source_target_pairs={{0,1},{1,2},{2,3},{3,4},{4,5},{5,6},{6,7}} | collective-permute-start | bytes 12296 | tf_op jit(solution)/shard_map/ppermute | solution.py:20
  32.2 5.9 %collective-permute-start.4 = (bf16[16,256]{1,0:T(8,128)(2,1)S(1)}, bf16[16,256]{1,0:T(8,128)(2,1)S(1)}, u32[]{:S(2)}, u32[]{:S(2)}) collective-permute-start(bf16[16,256]{1,0:T(8,128)(2,1)S(1)} %slice.734), channel_id=1, source_target_pairs={{0,1},{1,2},{2,3},{3,4},{4,5},{5,6},{6,7}} | collective-permute-start | bytes 24584 | tf_op jit(solution)/shard_map/ppermute | solution.py:20
  39.7 6.0 %collective-permute-start.5 = (bf16[32,256]{1,0:T(8,128)(2,1)S(1)}, bf16[32,256]{1,0:T(8,128)(2,1)S(1)}, u32[]{:S(2)}, u32[]{:S(2)}) collective-permute-start(bf16[32,256]{1,0:T(8,128)(2,1)S(1)} %slice.738), channel_id=1, source_target_pairs={{0,1},{1,2},{2,3},{3,4},{4,5},{5,6},{6,7}} | collective-permute-start | bytes 49160 | tf_op jit(solution)/shard_map/ppermute | solution.py:20
  47.3 6.1 %collective-permute-start.6 = (bf16[64,256]{1,0:T(8,128)(2,1)S(1)}, bf16[64,256]{1,0:T(8,128)(2,1)S(1)}, u32[]{:S(2)}, u32[]{:S(2)}) collective-permute-start(bf16[64,256]{1,0:T(8,128)(2,1)S(1)} %slice.742), channel_id=1, source_target_pairs={{0,1},{1,2},{2,3},{3,4},{4,5},{5,6},{6,7}} | collective-permute-start | bytes 98312 | tf_op jit(solution)/shard_map/ppermute | solution.py:20
  55.0 6.5 %collective-permute-start.7 = (bf16[128,256]{1,0:T(8,128)(2,1)S(1)}, bf16[128,256]{1,0:T(8,128)(2,1)S(1)}, u32[]{:S(2)}, u32[]{:S(2)}) collective-permute-start(bf16[128,256]{1,0:T(8,128)(2,1)S(1)} %slice.746), channel_id=1, source_target_pairs={{0,1},{1,2},{2,3},{3,4},{4,5},{5,6},{6,7}} | collective-permute-start | bytes 196616 | tf_op jit(solution)/shard_map/ppermute | solution.py:20
  63.1 7.2 %collective-permute-start.8 = (bf16[256,256]{1,0:T(8,128)(2,1)S(1)}, bf16[256,256]{1,0:T(8,128)(2,1)S(1)}, u32[]{:S(2)}, u32[]{:S(2)}) collective-permute-start(bf16[256,256]{1,0:T(8,128)(2,1)S(1)} %slice.750), channel_id=1, source_target_pairs={{0,1},{1,2},{2,3},{3,4},{4,5},{5,6},{6,7}} | collective-permute-start | bytes 393224 | tf_op jit(solution)/shard_map/ppermute | solution.py:20
  71.9 8.6 %collective-permute-start.9 = (bf16[512,256]{1,0:T(8,128)(2,1)S(1)}, bf16[512,256]{1,0:T(8,128)(2,1)S(1)}, u32[]{:S(2)}, u32[]{:S(2)}) collective-permute-start(bf16[512,256]{1,0:T(8,128)(2,1)S(1)} %get-tuple-element.4), channel_id=1, source_target_pairs={{0,1},{1,2},{2,3},{3,4},{4,5},{5,6},{6,7}} | collective-permute-start | bytes 786440 | tf_op jit(solution)/shard_map/ppermute | solution.py:20
  82.1 5.8 %collective-permute-start.10 = (bf16[1,256]{1,0:T(2,128)(2,1)S(1)}, bf16[1,256]{1,0:T(2,128)(2,1)S(1)}, u32[]{:S(2)}, u32[]{:S(2)}) collective-permute-start(bf16[1,256]{1,0:T(2,128)(2,1)S(1)} %slice.758), channel_id=1, source_target_pairs={{0,1},{1,2},{2,3},{3,4},{4,5},{5,6},{6,7}} | collective-permute-start | bytes 1544 | tf_op jit(solution)/shard_map/ppermute | solution.py:20
  89.5 5.8 %collective-permute-start.11 = (bf16[2,256]{1,0:T(2,128)(2,1)S(1)}, bf16[2,256]{1,0:T(2,128)(2,1)S(1)}, u32[]{:S(2)}, u32[]{:S(2)}) collective-permute-start(bf16[2,256]{1,0:T(2,128)(2,1)S(1)} %slice.762), channel_id=1, source_target_pairs={{0,1},{1,2},{2,3},{3,4},{4,5},{5,6},{6,7}} | collective-permute-start | bytes 3080 | tf_op jit(solution)/shard_map/ppermute | solution.py:20
  96.9 5.8 %collective-permute-start.12 = (bf16[4,256]{1,0:T(4,128)(2,1)S(1)}, bf16[4,256]{1,0:T(4,128)(2,1)S(1)}, u32[]{:S(2)}, u32[]{:S(2)}) collective-permute-start(bf16[4,256]{1,0:T(4,128)(2,1)S(1)} %slice.766), channel_id=1, source_target_pairs={{0,1},{1,2},{2,3},{3,4},{4,5},{5,6},{6,7}} | collective-permute-start | bytes 6152 | tf_op jit(solution)/shard_map/ppermute | solution.py:20
  104.4 5.8 %collective-permute-start.13 = (bf16[8,256]{1,0:T(8,128)(2,1)S(1)}, bf16[8,256]{1,0:T(8,128)(2,1)S(1)}, u32[]{:S(2)}, u32[]{:S(2)}) collective-permute-start(bf16[8,256]{1,0:T(8,128)(2,1)S(1)} %slice.770), channel_id=1, source_target_pairs={{0,1},{1,2},{2,3},{3,4},{4,5},{5,6},{6,7}} | collective-permute-start | bytes 12296 | tf_op jit(solution)/shard_map/ppermute | solution.py:20
  111.8 5.9 %collective-permute-start.14 = (bf16[16,256]{1,0:T(8,128)(2,1)S(1)}, bf16[16,256]{1,0:T(8,128)(2,1)S(1)}, u32[]{:S(2)}, u32[]{:S(2)}) collective-permute-start(bf16[16,256]{1,0:T(8,128)(2,1)S(1)} %slice.774), channel_id=1, source_target_pairs={{0,1},{1,2},{2,3},{3,4},{4,5},{5,6},{6,7}} | collective-permute-start | bytes 24584 | tf_op jit(solution)/shard_map/ppermute | solution.py:20
  119.2 6.0 %collective-permute-start.15 = (bf16[32,256]{1,0:T(8,128)(2,1)S(1)}, bf16[32,256]{1,0:T(8,128)(2,1)S(1)}, u32[]{:S(2)}, u32[]{:S(2)}) collective-permute-start(bf16[32,256]{1,0:T(8,128)(2,1)S(1)} %slice.778), channel_id=1, source_target_pairs={{0,1},{1,2},{2,3},{3,4},{4,5},{5,6},{6,7}} | collective-permute-start | bytes 49160 | tf_op jit(solution)/shard_map/ppermute | solution.py:20
  126.8 6.1 %collective-permute-start.16 = (bf16[64,256]{1,0:T(8,128)(2,1)S(1)}, bf16[64,256]{1,0:T(8,128)(2,1)S(1)}, u32[]{:S(2)}, u32[]{:S(2)}) collective-permute-start(bf16[64,256]{1,0:T(8,128)(2,1)S(1)} %slice.782), channel_id=1, source_target_pairs={{0,1},{1,2},{2,3},{3,4},{4,5},{5,6},{6,7}} | collective-permute-start | bytes 98312 | tf_op jit(solution)/shard_map/ppermute | solution.py:20
  134.5 6.5 %collective-permute-start.17 = (bf16[128,256]{1,0:T(8,128)(2,1)S(1)}, bf16[128,256]{1,0:T(8,128)(2,1)S(1)}, u32[]{:S(2)}, u32[]{:S(2)}) collective-permute-start(bf16[128,256]{1,0:T(8,128)(2,1)S(1)} %slice.786), channel_id=1, source_target_pairs={{0,1},{1,2},{2,3},{3,4},{4,5},{5,6},{6,7}} | collective-permute-start | bytes 196616 | tf_op jit(solution)/shard_map/ppermute | solution.py:20
  142.6 7.2 %collective-permute-start.18 = (bf16[256,256]{1,0:T(8,128)(2,1)S(1)}, bf16[256,256]{1,0:T(8,128)(2,1)S(1)}, u32[]{:S(2)}, u32[]{:S(2)}) collective-permute-start(bf16[256,256]{1,0:T(8,128)(2,1)S(1)} %slice.790), channel_id=1, source_target_pairs={{0,1},{1,2},{2,3},{3,4},{4,5},{5,6},{6,7}} | collective-permute-start | bytes 393224 | tf_op jit(solution)/shard_map/ppermute | solution.py:20
  151.4 8.6 %collective-permute-start.19 = (bf16[512,256]{1,0:T(8,128)(2,1)S(1)}, bf16[512,256]{1,0:T(8,128)(2,1)S(1)}, u32[]{:S(2)}, u32[]{:S(2)}) collective-permute-start(bf16[512,256]{1,0:T(8,128)(2,1)S(1)} %get-tuple-element.2), channel_id=1, source_target_pairs={{0,1},{1,2},{2,3},{3,4},{4,5},{5,6},{6,7}} | collective-permute-start | bytes 786440 | tf_op jit(solution)/shard_map/ppermute | solution.py:20
  (7 other events, 29.7 us)
where the time goes:
time: 166 us; the launch traced here: 165 us
  waiting for transfers between devices  79.7 us (48%)
  starting transfers between devices  39 us (23%)
  matrix products  34.6 us (21%)
  other arithmetic  8.32 us (5%)
  between operations  1.75 us (1%)
    ppermute x20, waiting for transfers between devices, local_stack(): halo_rows = lax.ppermute(hidden[-dilation:], 'sp', perm=shift_perm)  79.7 us
    ppermute x20, starting transfers between devices, local_stack(): halo_rows = lax.ppermute(hidden[-dilation:], 'sp', perm=shift_perm)  39 us
    dot_general x20, matrix products, local_stack(): jnp.dot(hidden, w_now[stack_idx, layer_pos], preferred_element_type=jnp.f...  9.8 us
    dot_general x20, matrix products, local_stack(): jnp.dot(shifted, w_past[stack_idx, layer_pos], preferred_element_type=jnp...  9.74 us
    convert_element_type x20, other arithmetic, local_stack(): (jnp.tanh(pre_act[:, :gate_ch]) * jax.nn.sigmoid(pre_act[:, gate_ch:])).a...  8.32 us
    dot_general x20, matrix products, local_stack(): jnp.dot(gated, w_res[stack_idx, layer_pos], preferred_element_type=jnp.fl...  6.72 us
    dot_general x19, matrix products, local_stack(): jnp.dot(gated, w_skip[stack_idx, layer_pos], preferred_element_type=jnp.f...  5.65 us
  transfers between devices with their start and end apart: 20, of which 20 were waited for; matrix products, arithmetic and copies ran while one was open for 5% of the time, Pallas kernels for 0%

commit v1 on v0

v1 whole, which is shorter than its diff:
```python
import dataclasses

import jax
import jax.numpy as jnp
from jax import lax
from jax.experimental import pallas as pl
from jax.experimental.pallas import tpu as pltpu
from jax.sharding import PartitionSpec as P

F32, BF16 = jnp.float32, jnp.bfloat16
ROWS, CH, LAYERS, CYCLE = 1024, 256, 20, 10
HALO = 512
PIECE = 64
XROWS = 128
EDGE = 128

LAT_Z, LAT_LINK, CYC_ROW = 750, 5200, 10.5


def dil(layer):
    return 2 ** (layer % CYCLE)


@dataclasses.dataclass
class Job:
    layer: int
    start: int
    rows: int
    valid: int
    needs: list = dataclasses.field(default_factory=list)
    halos: list = dataclasses.field(default_factory=list)
    path: float = 0.0

    @property
    def end(self):
        return self.start + self.rows

    @property
    def cost(self):
        return max(1.5 * self.rows * 1.15, 200)


@dataclasses.dataclass
class Head:
    start: int
    rows: int
    needs: list
    path: float = 0.0
    cost: float = 300.0


@dataclasses.dataclass
class Halo:
    layer: int
    start: int
    rows: int
    index: int = 0
    needs: list = dataclasses.field(default_factory=list)
    path: float = 0.0


def plan():
    jobs, halos = [], []

    def add(layer, start, rows, valid=None):
        jobs.append(Job(layer, start, rows, start if valid is None else valid))

    for layer in range(7):
        reach = 2 * dil(layer)
        for start in (768, 512, 256):
            add(layer, start, 256)
        if layer < 6:
            add(layer, 0, 256, reach - 1)
        else:
            add(layer, 64, 192, reach - 1)
        low, high = (-128, 64) if layer < 5 else (-64, 64) if layer == 5 else (0, 128)
        add(layer, low, high - low, reach - EDGE)
    for layer in (7, 8, 9, 17, 18):
        for start in (768, 512, 256, 0):
            add(layer, start, 256)
    for layer in range(10, 17):
        reach = 2 * dil(layer)
        add(layer, 768, 256)
        if layer < 16:
            add(layer, 512, 256, 512 + reach - 1)
            add(layer, 384, 192)
            add(layer, 256, 128, 256 + reach - 1)
            add(layer, 128, 192)
            low = -128 if layer < 15 else -64
            add(layer, low, 128 - low, reach - EDGE)
        else:
            add(layer, 576, 192, 512 + reach - 1)
            add(layer, 448, 192)
            add(layer, 320, 128, 256 + reach - 1)
            add(layer, 192, 192)
            add(layer, 0, 192)
    for start, rows in ((768, 256), (512, 256), (256, 256), (128, 128), (0, 128)):
        add(19, start, rows)

    for layer, rows, chunk in ((0, 128, 128), (7, 128, 128), (8, 256, 256), (9, 512, 256),
                               (10, 128, 128), (17, 128, 128), (18, 256, 256), (19, 512, 128)):
        for top in range(0, rows, chunk):
            halos.append(Halo(layer, -top - chunk, chunk, len(halos)))

    def cover(layer, low, high):
        if layer == 0 or high <= low:
            return []
        found, want = [], set(range(low, high))
        for j in [j for j in jobs if j.layer == layer - 1]:
            have = want & set(range(max(j.valid, j.start), j.end))
            if have:
                found.append(j)
                want -= have
        assert not want, (layer, low, high, sorted(want)[:3])
        return found

    for j in jobs:
        d = dil(j.layer)
        for low, high in ((j.valid, j.end), (j.valid - d, j.end - d)):
            inner = max(low, 0)
            if low < 0 and dil(j.layer) > 64 or low < 0 and j.layer % CYCLE == 0:
                j.halos += [h for h in halos if h.layer == j.layer and h.start < high and h.start + h.rows > low and h not in j.halos]
            elif low < 0:
                inner = low
            j.needs += [k for k in cover(j.layer, inner, high) if k not in j.needs]
    for j in jobs:
        j.needs += [k for k in jobs if k.layer == j.layer and k is not j and k.start < j.end and k.valid > j.start and k.valid > k.start
                    and k not in j.needs and (k.start, k.rows) != (j.start, j.rows) and j.valid < k.valid]
    for h in halos:
        h.needs = cover(h.layer, ROWS + h.start, ROWS + h.start + h.rows)

    heads = [Head(j.start, j.rows, [j] + [k for k in jobs if k.end > j.start and k.start < j.end and k.end > 0])
             for j in jobs if j.layer == LAYERS - 1]

    for head in heads:
        head.path = head.cost + LAT_Z
    for layer in range(LAYERS, -1, -1):
        for j in [j for j in jobs if j.layer == layer]:
            users = [k for k in jobs if k.layer == layer + 1 and j in k.needs]
            sent = [h for h in halos if j in h.needs]
            j.path = j.cost + LAT_Z + max([k.path for k in users] + [h.path for h in sent] + [600])
        for h in [h for h in halos if h.layer == layer]:
            h.path = LAT_LINK + CYC_ROW * h.rows + max(k.path for k in jobs if h in k.halos)

    now, order, done, arrive, link = 0.0, [], {}, {}, 0.0
    left = list(jobs) + heads
    while left:
        for h in halos:
            if h.index not in arrive and all(id(k) in done for k in h.needs):
                begin = max([link] + [done[id(k)] for k in h.needs])
                link = begin + CYC_ROW * h.rows
                arrive[h.index] = link + LAT_LINK
        best = None
        for i in left:
            if not all(id(k) in done for k in i.needs):
                continue
            hs = getattr(i, "halos", [])
            if not all(h.index in arrive for h in hs):
                continue
            ready = max([now] + [done[id(k)] for k in i.needs] + [arrive[h.index] for h in hs])
            key = (max(ready - now, 0), -i.path, -i.start)
            if best is None or key < best[0]:
                best = (key, i, ready)
        _, i, ready = best
        now = max(now, ready) + i.cost
        done[id(i)] = now + LAT_Z
        order.append(i)
        left = [k for k in left if k is not i]
    return order, halos, now


WEIGHT_WAITS = (0, 1, 2, 3, 5, 8, 13, 20)


def dot(a, b):
    return jnp.dot(a, b, preferred_element_type=F32)


def kernel(order, halos, devices, x, wp, wn, b, wr, ws, w1, b1, w2, b2, y, h_out,
           H, S, XH, W, WRS, W1, W2, B, B1, B2, wsem, osem, send_sem, recv_sem):
    me = lax.axis_index("sp")
    first = me == 0

    load_x = pltpu.make_async_copy(x, H.at[0, HALO:HALO + ROWS], wsem.at[LAYERS + 1])
    small = [pltpu.make_async_copy(src, dst, wsem.at[LAYERS + 2 + i])
             for i, (src, dst) in enumerate(((b, B), (b1, B1), (b2, B2)))]
    layer_loads = []
    for layer in range(LAYERS):
        layer_loads.append([pltpu.make_async_copy(wp.at[layer], W.at[layer, 0:CH], wsem.at[layer]),
                            pltpu.make_async_copy(wn.at[layer], W.at[layer, CH:2 * CH], wsem.at[layer]),
                            pltpu.make_async_copy(wr.at[layer], WRS.at[layer, :, 0:CH], wsem.at[layer]),
                            pltpu.make_async_copy(ws.at[layer], WRS.at[layer, :, CH:2 * CH], wsem.at[layer])])
    head_loads = [pltpu.make_async_copy(w1, W1, wsem.at[LAYERS]), pltpu.make_async_copy(w2, W2, wsem.at[LAYERS + 5])]
    for c in [load_x] + layer_loads[0] + small:
        c.start()
    for group in layer_loads[1:]:
        for c in group:
            c.start()
    for c in head_loads:
        c.start()

    @pl.when(first)
    def _():
        XH[...] = jnp.zeros_like(XH)
        for h in halos:
            if h.layer:
                H[h.layer, HALO + h.start:HALO + h.start + h.rows] = jnp.zeros((h.rows, CH), BF16)

    barrier = pltpu.get_barrier_semaphore()

    @pl.when(me > 0)
    def _():
        pl.semaphore_signal(barrier, inc=1, device_id={"sp": me - 1}, device_id_type=pl.DeviceIdType.MESH)

    @pl.when(me < devices - 1)
    def _():
        pl.semaphore_wait(barrier, 1)

    def remote(h):
        src = H.at[h.layer, HALO + ROWS + h.start:HALO + ROWS + h.start + h.rows]
        dst = H.at[h.layer, HALO + h.start:HALO + h.start + h.rows] if h.layer else XH.at[XROWS + h.start:XROWS + h.start + h.rows]
        return pltpu.make_async_remote_copy(
            src_ref=src, dst_ref=dst, send_sem=send_sem.at[h.index], recv_sem=recv_sem.at[h.index],
            device_id={"sp": lax.rem(me + 1, devices)}, device_id_type=pl.DeviceIdType.MESH)

    finished, sent, arrived, weighed, added, reads = set(), set(), set(), set(), set(), []

    def wait_for(item):
        if isinstance(item, Job):
            if item.layer not in weighed:
                low = max(k for k in WEIGHT_WAITS if k <= item.layer)
                high = min(k for k in WEIGHT_WAITS if k > item.layer)
                for layer in range(low, high):
                    weighed.add(layer)
                    for c in layer_loads[layer]:
                        c.wait()
            for h in item.halos:
                if h.index not in arrived:
                    arrived.add(h.index)
                    pl.when(me > 0)(remote(h).wait_recv)
                    if not h.layer:
                        H[0, HALO + h.start:HALO + h.start + h.rows] = XH[XROWS + h.start:XROWS + h.start + h.rows]
        elif isinstance(item, Head) and "head" not in weighed:
            weighed.add("head")
            for c in head_loads:
                c.wait()

    def send_ready():
        for h in halos:
            if h.index not in sent and all(id(k) in finished for k in h.needs):
                sent.add(h.index)
                pl.when(me < devices - 1)(remote(h).start)

    def write_back(src, dst, index):
        c = pltpu.make_async_copy(src, dst, osem.at[index])
        c.start()
        reads.append(c)

    def z_stage(item):
        at, d = HALO + item.start, dil(item.layer)
        both = jnp.concatenate([H[item.layer, at - d:at - d + item.rows], H[item.layer, at:at + item.rows]], axis=1)
        return dot(both, W[item.layer])

    def gate_stage(item, z):
        z = z + B[item.layer // CYCLE, item.layer % CYCLE:item.layer % CYCLE + 1]
        t = jnp.tanh(z[:, :CH])
        u = jnp.tanh(0.5 * z[:, CH:])
        return (0.5 * (t * u + t)).astype(BF16)

    def fin_stage(item, g):
        at = HALO + item.start
        rs = dot(g, WRS[item.layer])
        new = (H[item.layer, at:at + item.rows].astype(F32) + rs[:, :CH]).astype(BF16)
        if item.start < 0:
            cut = min(-item.start, item.rows)
            top = jnp.where(first, jnp.zeros((cut, CH), BF16), new[:cut])
            H[item.layer + 1, at:at + cut] = top
            if cut < item.rows:
                H[item.layer + 1, at + cut:at + item.rows] = new[cut:]
        else:
            H[item.layer + 1, at:at + item.rows] = new
        fresh = [i for i in range(0, item.rows, PIECE)
                 if item.start + i >= max(item.valid, 0) and (item.layer, item.start + i) not in added]
        added.update((item.layer, item.start + i) for i in fresh)
        if fresh:
            low, high = fresh[0], fresh[-1] + PIECE
            assert high - low == len(fresh) * PIECE
            rows = slice(item.start + low, item.start + high)
            part = rs[low:high, CH:]
            S[rows] = part if item.layer == 0 else S[rows] + part
        finished.add(id(item))

    pipe = []

    def retire(upto):
        while len(pipe) > upto:
            item, z = pipe.pop(0)
            fin_stage(item, gate_stage(item, z))
            if item.layer == LAYERS - 1:
                write_back(H.at[LAYERS, HALO + item.start:HALO + item.end], h_out.at[item.start:item.end], len(reads))
            send_ready()

    def head_stage(item):
        rows = slice(item.start, item.start + item.rows)
        a = jnp.maximum(S[rows], 0.0).astype(BF16)
        m = jnp.maximum(dot(a, W1[...]) + B1[...], 0.0).astype(BF16)
        S[rows] = dot(m, W2[...]) + B2[...]
        write_back(S.at[item.start:item.start + item.rows], y.at[item.start:item.start + item.rows], len(reads))

    load_x.wait()
    send_ready()
    for c in small:
        c.wait()
    for item in order:
        while pipe and not all(id(k) in finished for k in item.needs):
            retire(len(pipe) - 1)
        assert all(id(k) in finished for k in item.needs)
        wait_for(item)
        if isinstance(item, Head):
            head_stage(item)
            continue
        pipe.append((item, z_stage(item)))
        retire(1)
    retire(0)
    for c in reads:
        c.wait()

    @pl.when(me < devices - 1)
    def _():
        for h in halos:
            remote(h).wait_send()


def solution(mesh):
    devices = mesh.shape["sp"]
    order, halos, _ = plan()
    rows = P(("ens", "sp"), None)
    outs = sum(isinstance(i, Head) for i in order) + sum(isinstance(i, Job) and i.layer == LAYERS - 1 for i in order)

    def local(x, wp, wn, b, wr, ws, w1, b1, w2, b2):
        hbm = pl.BlockSpec(memory_space=pltpu.HBM)
        vmem = lambda *shape: pltpu.VMEM(shape, BF16)
        return pl.pallas_call(
            lambda *refs: kernel(order, halos, devices, *refs),
            out_shape=(jax.ShapeDtypeStruct((ROWS, CH), F32), jax.ShapeDtypeStruct((ROWS, CH), BF16)),
            in_specs=[hbm] * 10,
            out_specs=(hbm, hbm),
            scratch_shapes=[
                vmem(LAYERS + 1, HALO + ROWS, CH), pltpu.VMEM((ROWS, CH), F32), vmem(XROWS, CH),
                vmem(LAYERS, 2 * CH, 2 * CH), vmem(LAYERS, CH, 2 * CH), vmem(CH, CH), vmem(CH, CH),
                pltpu.VMEM((LAYERS // CYCLE, CYCLE, 2 * CH), F32), pltpu.VMEM((1, CH), F32), pltpu.VMEM((1, CH), F32),
                pltpu.SemaphoreType.DMA((LAYERS + 6,)), pltpu.SemaphoreType.DMA((outs,)),
                pltpu.SemaphoreType.DMA((len(halos),)), pltpu.SemaphoreType.DMA((len(halos),)),
            ],
            compiler_params=pltpu.CompilerParams(collective_id=0, has_side_effects=True, vmem_limit_bytes=62 * 1024 * 1024),
            name="wavenet_stack",
        )(x, wp.reshape(LAYERS, CH, 2 * CH), wn.reshape(LAYERS, CH, 2 * CH), b,
          wr.reshape(LAYERS, CH, CH), ws.reshape(LAYERS, CH, CH), w1, b1.reshape(1, CH), w2, b2.reshape(1, CH))

    return jax.shard_map(local, mesh=mesh, in_specs=(rows,) + (P(),) * 9, out_specs=(rows, rows), check_vma=False)
```

time: 166 us -> 44.6 us (0.27)
  waiting for transfers between devices: 79.7 us -> 0 us
  starting transfers between devices: 39 us -> 0 us
  Pallas kernels: 0 us -> 38.1 us
  matrix products: 34.6 us -> 0 us
  other arithmetic: 8.32 us -> 0 us
  local copies, waits for them, and re-layouts: 1.43 us -> 5.55 us
    ppermute x20 -> x0, waiting for transfers between devices: 79.7 us -> none  [local_stack(): halo_rows = lax.ppermute(hidden[-dilation:], 'sp', perm=shift_perm)]
    ppermute x20 -> x0, starting transfers between devices: 39 us -> none  [local_stack(): halo_rows = lax.ppermute(hidden[-dilation:], 'sp', perm=shift_perm)]
    pallas_call x0 -> x1, Pallas kernels: none -> 38.1 us  [local(): pl.pallas_call(lambda *refs: kernel(order, halos, devices, *refs), out_sh...]
    dot_general x81 -> x0, matrix products: 34.6 us -> none  [the longest x20 9.8 us: local_stack(): jnp.dot(hidden, w_now[stack_idx, layer_pos], preferred_element_type=jnp.f...]
    convert_element_type x20 -> x0, other arithmetic: 8.32 us -> none  [local_stack(): (jnp.tanh(pre_act[:, :gate_ch]) * jax.nn.sigmoid(pre_act[:, gate_ch:])).a...]
    unnamed x22 -> x3, local copies, waits for them, and re-layouts: 0.07 us -> 5.55 us
  transfers between devices with their start and end apart: 20 -> 0, of which waited for: 20 -> 0; matrix products, arithmetic and copies ran while one was open for 5% -> 0% of each run, Pallas kernels for 0% -> 0%
where the time goes in v1:
time: 44.6 us; the launch traced here: 44.3 us
  Pallas kernels  38.1 us (85%)
  local copies, waits for them, and re-layouts  5.55 us (12%)
  between operations  0.64 us (1%)
    pallas_call x1, Pallas kernels, local(): pl.pallas_call(lambda *refs: kernel(order, halos, devices, *refs), out_sh...  38.1 us
    unnamed x3, local copies, waits for them, and re-layouts  5.55 us

profile of v1, /device:TPU:4, one launch (start us, length us, event | category | flops | bytes accessed | tf_op | source)
XLA Modules:
  0.0 44.3 jit_solution(15720487541682216144)
XLA Ops:
  0.6 1.4 %copy.12.refs_3_ = f32[2,10,512]{2,1,0:T(8,128)} copy(f32[2,10,512]{2,0,1:T(2,128)} %param.13) | data formatting | bytes 81920 | tf_op args[3]
  2.0 38.1 %wavenet_stack.1 = (f32[1024,256]{1,0:T(8,128)}, bf16[1024,256]{1,0:T(8,128)(2,1)}) custom-call(bf16[1024,256]{1,0:T(8,128)(2,1)} %refs_0_.1, bf16[20,256,512]{2,1,0:T(8,128)(2,1)} %bitcast.6, bf16[20,256,512]{2,1,0:T(8,128)(2,1)} %bitcast.7, f32[2,10,512]{2,1,0:T(8,128)} %copy.12.refs_3_, bf16[20,256,256]{2,1,0:T(8,128)(2,1)} %bitcast.8, ...), custom_call_target="tpu_custom_call" | custom-call | tf_op jit(solution)/shard_map/wavenet_stack/pallas_call | solution.py:343
  40.1 2.3 %copy.15 = f32[1024,256]{1,0:T(8,128)} copy(f32[1024,256]{1,0:T(8,128)} %get-tuple-element.4) | data formatting | bytes 2097152
  42.4 1.9 %copy.16 = bf16[1024,256]{1,0:T(8,128)(2,1)} copy(bf16[1024,256]{1,0:T(8,128)(2,1)} %get-tuple-element.5) | data formatting | bytes 1048576

commit v2 on v1

--- a/solution.py
+++ b/solution.py
@@ -38,15 +38,6 @@
     @property
     def cost(self):
         return max(1.5 * self.rows * 1.15, 200)
-
-
-@dataclasses.dataclass
-class Head:
-    start: int
-    rows: int
-    needs: list
-    path: float = 0.0
-    cost: float = 300.0
 
 
 @dataclasses.dataclass
@@ -129,11 +120,6 @@
     for h in halos:
         h.needs = cover(h.layer, ROWS + h.start, ROWS + h.start + h.rows)
 
-    heads = [Head(j.start, j.rows, [j] + [k for k in jobs if k.end > j.start and k.start < j.end and k.end > 0])
-             for j in jobs if j.layer == LAYERS - 1]
-
-    for head in heads:
-        head.path = head.cost + LAT_Z
     for layer in range(LAYERS, -1, -1):
         for j in [j for j in jobs if j.layer == layer]:
             users = [k for k in jobs if k.layer == layer + 1 and j in k.needs]
@@ -143,7 +129,7 @@
             h.path = LAT_LINK + CYC_ROW * h.rows + max(k.path for k in jobs if h in k.halos)
 
     now, order, done, arrive, link = 0.0, [], {}, {}, 0.0
-    left = list(jobs) + heads
+    left = list(jobs)
     while left:
         for h in halos:
             if h.index not in arrive and all(id(k) in done for k in h.needs):
@@ -169,6 +155,7 @@
     return order, halos, now
 
 
+HEAD_ROWS = 256
 WEIGHT_WAITS = (0, 1, 2, 3, 5, 8, 13, 20)
 
 
@@ -176,28 +163,24 @@
     return jnp.dot(a, b, preferred_element_type=F32)
 
 
-def kernel(order, halos, devices, x, wp, wn, b, wr, ws, w1, b1, w2, b2, y, h_out,
-           H, S, XH, W, WRS, W1, W2, B, B1, B2, wsem, osem, send_sem, recv_sem):
+def stack_kernel(order, halos, devices, x, wp, wn, b, wr, ws, S, h_out,
+                 H, XH, W, WRS, B, wsem, send_sem, recv_sem):
     me = lax.axis_index("sp")
     first = me == 0
 
     load_x = pltpu.make_async_copy(x, H.at[0, HALO:HALO + ROWS], wsem.at[LAYERS + 1])
-    small = [pltpu.make_async_copy(src, dst, wsem.at[LAYERS + 2 + i])
-             for i, (src, dst) in enumerate(((b, B), (b1, B1), (b2, B2)))]
+    load_b = pltpu.make_async_copy(b, B, wsem.at[LAYERS])
     layer_loads = []
     for layer in range(LAYERS):
         layer_loads.append([pltpu.make_async_copy(wp.at[layer], W.at[layer, 0:CH], wsem.at[layer]),
                             pltpu.make_async_copy(wn.at[layer], W.at[layer, CH:2 * CH], wsem.at[layer]),
                             pltpu.make_async_copy(wr.at[layer], WRS.at[layer, :, 0:CH], wsem.at[layer]),
                             pltpu.make_async_copy(ws.at[layer], WRS.at[layer, :, CH:2 * CH], wsem.at[layer])])
-    head_loads = [pltpu.make_async_copy(w1, W1, wsem.at[LAYERS]), pltpu.make_async_copy(w2, W2, wsem.at[LAYERS + 5])]
-    for c in [load_x] + layer_loads[0] + small:
+    for c in [load_x] + layer_loads[0] + [load_b]:
         c.start()
     for group in layer_loads[1:]:
         for c in group:
             c.start()
-    for c in head_loads:
-        c.start()
 
     @pl.when(first)
     def _():
@@ -223,10 +206,10 @@
             src_ref=src, dst_ref=dst, send_sem=send_sem.at[h.index], recv_sem=recv_sem.at[h.index],
             device_id={"sp": lax.rem(me + 1, devices)}, device_id_type=pl.DeviceIdType.MESH)
 
-    finished, sent, arrived, weighed, added, reads = set(), set(), set(), set(), set(), []
+    finished, sent, arrived, weighed, added = set(), set(), set(), set(), set()
 
     def wait_for(item):
-        if isinstance(item, Job):
+        if item is not None:
             if item.layer not in weighed:
                 low = max(k for k in WEIGHT_WAITS if k <= item.layer)
                 high = min(k for k in WEIGHT_WAITS if k > item.layer)
@@ -240,10 +223,6 @@
                     pl.when(me > 0)(remote(h).wait_recv)
                     if not h.layer:
                         H[0, HALO + h.start:HALO + h.start + h.rows] = XH[XROWS + h.start:XROWS + h.start + h.rows]
-        elif isinstance(item, Head) and "head" not in weighed:
-            weighed.add("head")
-            for c in head_loads:
-                c.wait()
 
     def send_ready():
         for h in halos:
@@ -251,11 +230,6 @@
                 sent.add(h.index)
                 pl.when(me < devices - 1)(remote(h).start)
 
-    def write_back(src, dst, index):
-        c = pltpu.make_async_copy(src, dst, osem.at[index])
-        c.start()
-        reads.append(c)
-
     def z_stage(item):
         at, d = HALO + item.start, dil(item.layer)
         both = jnp.concatenate([H[item.layer, at - d:at - d + item.rows], H[item.layer, at:at + item.rows]], axis=1)
@@ -267,9 +241,8 @@
         u = jnp.tanh(0.5 * z[:, CH:])
         return (0.5 * (t * u + t)).astype(BF16)
 
-    def fin_stage(item, g):
+    def fin_stage(item, rs):
         at = HALO + item.start
-        rs = dot(g, WRS[item.layer])
         new = (H[item.layer, at:at + item.rows].astype(F32) + rs[:, :CH]).astype(BF16)
         if item.start < 0:
             cut = min(-item.start, item.rows)
@@ -277,8 +250,10 @@
             H[item.layer + 1, at:at + cut] = top
             if cut < item.rows:
                 H[item.layer + 1, at + cut:at + item.rows] = new[cut:]
+        elif item.layer < LAYERS - 1:
+            H[item.layer + 1, at:at + item.rows] = new
         else:
-            H[item.layer + 1, at:at + item.rows] = new
+            h_out[item.start:item.end] = new
         fresh = [i for i in range(0, item.rows, PIECE)
                  if item.start + i >= max(item.valid, 0) and (item.layer, item.start + i) not in added]
         added.update((item.layer, item.start + i) for i in fresh)
@@ -292,38 +267,28 @@
 
     pipe = []
 
-    def retire(upto):
-        while len(pipe) > upto:
-            item, z = pipe.pop(0)
-            fin_stage(item, gate_stage(item, z))
-            if item.layer == LAYERS - 1:
-                write_back(H.at[LAYERS, HALO + item.start:HALO + item.end], h_out.at[item.start:item.end], len(reads))
-            send_ready()
-
-    def head_stage(item):
-        rows = slice(item.start, item.start + item.rows)
-        a = jnp.maximum(S[rows], 0.0).astype(BF16)
-        m = jnp.maximum(dot(a, W1[...]) + B1[...], 0.0).astype(BF16)
-        S[rows] = dot(m, W2[...]) + B2[...]
-        write_back(S.at[item.start:item.start + item.rows], y.at[item.start:item.start + item.rows], len(reads))
+    def step(item, coming):
+        g = gate_stage(item, z_stage(item)) if item is not None else None
+        send_ready()
+        wait_for(coming)
+        if pipe:
+            done, gated = pipe.pop()
+            fin_stage(done, dot(gated, WRS[done.layer]))
+        if item is not None:
+            pipe.append((item, g))
 
     load_x.wait()
     send_ready()
-    for c in small:
-        c.wait()
-    for item in order:
-        while pipe and not all(id(k) in finished for k in item.needs):
-            retire(len(pipe) - 1)
-        assert all(id(k) in finished for k in item.needs)
-        wait_for(item)
-        if isinstance(item, Head):
-            head_stage(item)
-            continue
-        pipe.append((item, z_stage(item)))
-        retire(1)
-    retire(0)
-    for c in reads:
-        c.wait()
+    load_b.wait()
+    wait_for(order[0])
+    for n, item in enumerate(order):
+        while not all(id(k) in finished for k in item.needs):
+            assert pipe
+            step(None, item)
+        coming = order[n + 1] if n + 1 < len(order) else None
+        step(item, coming)
+    while pipe:
+        step(None, None)
 
     @pl.when(me < devices - 1)
     def _():
@@ -331,30 +296,55 @@
             remote(h).wait_send()
 
 
+def head_kernel(S, h, w1, b1, w2, b2, y, h_out, Y, sem):
+    pass_h = pltpu.make_async_copy(h, h_out, sem.at[0])
+    pass_h.start()
+    writes = []
+    for n, start in enumerate(range(0, ROWS, HEAD_ROWS)):
+        rows = slice(start, start + HEAD_ROWS)
+        a = jnp.maximum(S[rows], 0.0).astype(BF16)
+        m = jnp.maximum(dot(a, w1[...]) + b1[...], 0.0).astype(BF16)
+        Y[rows] = dot(m, w2[...]) + b2[...]
+        c = pltpu.make_async_copy(Y.at[rows], y.at[rows], sem.at[1 + n])
+        c.start()
+        writes.append(c)
+    pass_h.wait()
+    for c in writes:
+        c.wait()
+
+
 def solution(mesh):
     devices = mesh.shape["sp"]
     order, halos, _ = plan()
     rows = P(("ens", "sp"), None)
-    outs = sum(isinstance(i, Head) for i in order) + sum(isinstance(i, Job) and i.layer == LAYERS - 1 for i in order)
 
     def local(x, wp, wn, b, wr, ws, w1, b1, w2, b2):
-        hbm = pl.BlockSpec(memory_space=pltpu.HBM)
+        hbm, near = pl.BlockSpec(memory_space=pltpu.HBM), pl.BlockSpec(memory_space=pltpu.VMEM)
         vmem = lambda *shape: pltpu.VMEM(shape, BF16)
-        return pl.pallas_call(
-            lambda *refs: kernel(order, halos, devices, *refs),
-            out_shape=(jax.ShapeDtypeStruct((ROWS, CH), F32), jax.ShapeDtypeStruct((ROWS, CH), BF16)),
-            in_specs=[hbm] * 10,
-            out_specs=(hbm, hbm),
+        skip, hidden = pl.pallas_call(
+            lambda *refs: stack_kernel(order, halos, devices, *refs),
+            out_shape=(pltpu.VMEM((ROWS, CH), F32), pltpu.VMEM((ROWS, CH), BF16)),
+            in_specs=[hbm] * 6,
+            out_specs=(near, near),
             scratch_shapes=[
-                vmem(LAYERS + 1, HALO + ROWS, CH), pltpu.VMEM((ROWS, CH), F32), vmem(XROWS, CH),
-                vmem(LAYERS, 2 * CH, 2 * CH), vmem(LAYERS, CH, 2 * CH), vmem(CH, CH), vmem(CH, CH),
-                pltpu.VMEM((LAYERS // CYCLE, CYCLE, 2 * CH), F32), pltpu.VMEM((1, CH), F32), pltpu.VMEM((1, CH), F32),
-                pltpu.SemaphoreType.DMA((LAYERS + 6,)), pltpu.SemaphoreType.DMA((outs,)),
+                vmem(LAYERS, HALO + ROWS, CH), vmem(XROWS, CH),
+                vmem(LAYERS, 2 * CH, 2 * CH), vmem(LAYERS, CH, 2 * CH),
+                pltpu.VMEM((LAYERS // CYCLE, CYCLE, 2 * CH), F32),
+                pltpu.SemaphoreType.DMA((LAYERS + 2,)),
                 pltpu.SemaphoreType.DMA((len(halos),)), pltpu.SemaphoreType.DMA((len(halos),)),
             ],
-            compiler_params=pltpu.CompilerParams(collective_id=0, has_side_effects=True, vmem_limit_bytes=62 * 1024 * 1024),
+            compiler_params=pltpu.CompilerParams(collective_id=0, has_side_effects=True, vmem_limit_bytes=56 * 1024 * 1024),
             name="wavenet_stack",
         )(x, wp.reshape(LAYERS, CH, 2 * CH), wn.reshape(LAYERS, CH, 2 * CH), b,
-          wr.reshape(LAYERS, CH, CH), ws.reshape(LAYERS, CH, CH), w1, b1.reshape(1, CH), w2, b2.reshape(1, CH))
+          wr.reshape(LAYERS, CH, CH), ws.reshape(LAYERS, CH, CH))
+        return pl.pallas_call(
+            head_kernel,
+            out_shape=(jax.ShapeDtypeStruct((ROWS, CH), F32), jax.ShapeDtypeStruct((ROWS, CH), BF16)),
+            in_specs=[near] * 6,
+            out_specs=(hbm, hbm),
+            scratch_shapes=[pltpu.VMEM((ROWS, CH), F32), pltpu.SemaphoreType.DMA((1 + ROWS // HEAD_ROWS,))],
+            compiler_params=pltpu.CompilerParams(vmem_limit_bytes=6 * 1024 * 1024),
+            name="wavenet_head",
+        )(skip, hidden, w1, b1.reshape(1, CH), w2, b2.reshape(1, CH))
 
     return jax.shard_map(local, mesh=mesh, in_specs=(rows,) + (P(),) * 9, out_specs=(rows, rows), check_vma=False)

time: 44.6 us -> 33.7 us (0.76)
  Pallas kernels: 38.1 us -> 31.3 us
  local copies, waits for them, and re-layouts: 5.55 us -> 1.43 us
    pallas_call x1 -> x2, Pallas kernels: 38.1 us -> 31.3 us  [the longest x1 30 us: local(): pl.pallas_call(lambda *refs: stack_kernel(order, halos, devices, *refs),...]
    unnamed x3 -> x9, local copies, waits for them, and re-layouts: 5.55 us -> 1.43 us
where the time goes in v2:
time: 33.7 us; the launch traced here: 33.6 us
  Pallas kernels  31.3 us (93%)
  local copies, waits for them, and re-layouts  1.43 us (4%)
  between operations  0.83 us (2%)
    pallas_call x1, Pallas kernels, local(): pl.pallas_call(lambda *refs: stack_kernel(order, halos, devices, *refs),...  30 us
    unnamed x9, local copies, waits for them, and re-layouts  1.43 us
    pallas_call x1, Pallas kernels, local(): pl.pallas_call(head_kernel, out_shape=(jax.ShapeDtypeStruct((ROWS, CH), F...  1.35 us

profile of v2, /device:TPU:4, one launch (start us, length us, event | category | flops | bytes accessed | tf_op | source)
XLA Modules:
  0.0 33.6 jit_solution(10273045223538961675)
XLA Ops:
  0.6 1.4 %copy.12.refs_3_ = f32[2,10,512]{2,1,0:T(8,128)} copy(f32[2,10,512]{2,0,1:T(2,128)} %param.13) | data formatting | bytes 81920 | tf_op args[3]
  2.0 0.0 copy-start
  2.1 0.0 copy-start.1
  2.1 0.0 copy-start.2
  2.1 0.0 copy-start.3
  2.1 30.0 %wavenet_stack.1 = (f32[1024,256]{1,0:T(8,128)S(1)}, bf16[1024,256]{1,0:T(8,128)(2,1)S(1)}) custom-call(bf16[1024,256]{1,0:T(8,128)(2,1)} %refs_0_.1, bf16[20,256,512]{2,1,0:T(8,128)(2,1)} %bitcast.8, bf16[20,256,512]{2,1,0:T(8,128)(2,1)} %bitcast.9, f32[2,10,512]{2,1,0:T(8,128)} %copy.12.refs_3_, bf16[20,256,256]{2,1,0:T(8,128)(2,1)} %bitcast.10, ...), custom_call_target="tpu_custom_call" | custom-call | tf_op jit(solution)/shard_map/wavenet_stack/pallas_call | solution.py:324
  32.0 0.0 copy-done
  32.0 0.0 copy-done.1
  32.0 0.0 copy-done.2
  32.0 0.0 copy-done.3
  32.1 1.3 %wavenet_head.1 = (f32[1024,256]{1,0:T(8,128)}, bf16[1024,256]{1,0:T(8,128)(2,1)}) custom-call(f32[1024,256]{1,0:T(8,128)S(1)} %get-tuple-element.4.S, bf16[1024,256]{1,0:T(8,128)(2,1)S(1)} %get-tuple-element.5.h, bf16[256,256]{1,0:T(8,128)(2,1)S(1)} %copy-done, f32[1,256]{1,0:T(1,128)S(1)} %bitcast.6, bf16[256,256]{1,0:T(8,128)(2,1)S(1)} %copy-done.1, ...), custom_call_target="tpu_custom_call" | custom-call | tf_op jit(solution)/shard_map/wavenet_head/pallas_call | solution.py:340
Async XLA Ops:
  2.0 30.0 %copy-start = (bf16[256,256]{1,0:T(8,128)(2,1)S(1)}, bf16[256,256]{1,0:T(8,128)(2,1)}, u32[]{:S(2)}) copy-start(bf16[256,256]{1,0:T(8,128)(2,1)} %w1.1) | copy-start | bytes 393220
  2.1 30.0 %copy-start.1 = (bf16[256,256]{1,0:T(8,128)(2,1)S(1)}, bf16[256,256]{1,0:T(8,128)(2,1)}, u32[]{:S(2)}) copy-start(bf16[256,256]{1,0:T(8,128)(2,1)} %w2.1) | copy-start | bytes 393220
  2.1 30.0 %copy-start.2 = (f32[256]{0:T(256)S(1)}, f32[256]{0:T(256)}, u32[]{:S(2)}) copy-start(f32[256]{0:T(256)} %param.17) | copy-start | bytes 3076
  2.1 30.0 %copy-start.3 = (f32[256]{0:T(256)S(1)}, f32[256]{0:T(256)}, u32[]{:S(2)}) copy-start(f32[256]{0:T(256)} %param.19) | copy-start | bytes 3076

commit v3 on v0

v3 whole, which is shorter than its diff:
```python
import dataclasses

import jax
import jax.numpy as jnp
from jax import lax
from jax.experimental import pallas as pl
from jax.experimental.pallas import tpu as pltpu
from jax.sharding import PartitionSpec as P

F32, BF16 = jnp.float32, jnp.bfloat16
ROWS, CH, LAYERS, CYCLE = 1024, 256, 20, 10
HALO = 512
XROWS = 128
TILE = 256


def dil(layer):
    return 2 ** (layer % CYCLE)


@dataclasses.dataclass(frozen=True)
class Job:
    layer: int
    start: int
    rows: int
    needs: tuple
    halos: tuple

    @property
    def end(self):
        return self.start + self.rows


@dataclasses.dataclass(frozen=True)
class Halo:
    layer: int
    start: int
    rows: int
    index: int
    needs: tuple


JOBS = (
    (0, 768, 256, (), ()), (0, 512, 256, (), ()), (0, 256, 256, (), ()),
    (0, 0, 256, (), ()), (0, -128, 192, (3,), (0,)), (1, 768, 256, (0, 1), ()),
    (1, 512, 256, (1, 2), ()), (1, 256, 256, (2, 3), ()), (1, 0, 256, (3,), ()),
    (1, -128, 192, (3, 4, 8), ()), (2, 768, 256, (5, 6), ()), (2, 512, 256, (6, 7), ()),
    (2, 256, 256, (7, 8), ()), (2, 0, 256, (8,), ()), (2, -128, 192, (8, 9, 13), ()),
    (3, 768, 256, (10, 11), ()), (3, 512, 256, (11, 12), ()), (3, 256, 256, (12, 13), ()),
    (3, 0, 256, (13,), ()), (3, -128, 192, (13, 14, 18), ()), (4, 768, 256, (15, 16), ()),
    (4, 512, 256, (16, 17), ()), (4, 256, 256, (17, 18), ()), (4, 0, 256, (18,), ()),
    (4, -128, 192, (18, 19, 23), ()), (5, 768, 256, (20, 21), ()), (5, 512, 256, (21, 22), ()),
    (5, 256, 256, (22, 23), ()), (5, 0, 256, (23,), ()), (5, -64, 128, (23, 24, 28), ()),
    (6, 768, 256, (25, 26), ()), (6, 512, 256, (26, 27), ()), (6, 256, 256, (27, 28), ()),
    (6, 64, 192, (28,), ()), (6, 0, 128, (28, 29, 33), ()), (7, 768, 256, (30, 31), ()),
    (7, 512, 256, (31, 32), ()), (7, 256, 256, (32, 33), ()), (7, 0, 256, (33, 34), (1,)),
    (8, 768, 256, (35, 36), ()), (8, 512, 256, (36, 37), ()), (8, 256, 256, (37, 38), ()),
    (8, 0, 256, (38,), (2,)), (9, 768, 256, (39, 41), ()), (9, 512, 256, (40, 42), ()),
    (9, 256, 256, (41,), (3,)), (9, 0, 256, (42,), (4,)), (17, 768, 256, (91, 92), ()),
    (17, 512, 256, (92, 93, 94), ()), (17, 256, 256, (93, 94, 95, 96), ()), (17, 0, 256, (95, 96), (6,)),
    (18, 768, 256, (47, 48), ()), (18, 512, 256, (48, 49), ()), (18, 256, 256, (49, 50), ()),
    (18, 0, 256, (50,), (7,)), (10, 768, 256, (43, 44), ()), (10, 512, 256, (44,), ()),
    (10, 384, 192, (44, 45, 56), ()), (10, 256, 128, (45,), ()), (10, 64, 256, (45, 46, 58), ()),
    (10, -128, 192, (46,), (5,)), (11, 768, 256, (55, 56), ()), (11, 512, 256, (56,), ()),
    (11, 384, 192, (56, 57, 58, 62), ()), (11, 256, 128, (58,), ()), (11, 64, 256, (58, 59, 60, 64), ()),
    (11, -128, 192, (60,), ()), (12, 768, 256, (61, 62), ()), (12, 512, 256, (62,), ()),
    (12, 384, 192, (62, 63, 64, 68), ()), (12, 256, 128, (64,), ()), (12, 64, 256, (64, 65, 66, 70), ()),
    (12, -128, 192, (66,), ()), (13, 768, 256, (67, 68), ()), (13, 512, 256, (68,), ()),
    (13, 384, 192, (68, 69, 70, 74), ()), (13, 256, 128, (70,), ()), (13, 64, 256, (70, 71, 72, 76), ()),
    (13, -128, 192, (72,), ()), (14, 768, 256, (73, 74), ()), (14, 512, 256, (74,), ()),
    (14, 384, 192, (74, 75, 76, 80), ()), (14, 256, 128, (76,), ()), (14, 64, 256, (76, 77, 78, 82), ()),
    (14, -128, 192, (78,), ()), (15, 768, 256, (79, 80), ()), (15, 512, 256, (80,), ()),
    (15, 384, 192, (80, 81, 82, 86), ()), (15, 256, 128, (82,), ()), (15, 128, 192, (82, 83, 88), ()),
    (15, -64, 192, (83, 84), ()), (16, 768, 256, (85, 86), ()), (16, 576, 192, (86,), ()),
    (16, 448, 192, (86, 87, 92), ()), (16, 320, 128, (87, 88), ()), (16, 192, 192, (88, 89, 94), ()),
    (16, 0, 192, (89, 90), ()), (19, 768, 256, (51, 53), ()), (19, 512, 256, (52, 54), ()),
    (19, 256, 256, (53,), (8, 9)), (19, 128, 128, (54,), (10,)), (19, 0, 128, (54,), (11,)),
)
HALOS = (
    (0, -128, 128, ()), (7, -128, 128, (30,)), (8, -256, 256, (35,)),
    (9, -256, 256, (39,)), (9, -512, 256, (40,)), (10, -128, 128, (43,)),
    (17, -128, 128, (91,)), (18, -256, 256, (47,)), (19, -128, 128, (51,)),
    (19, -256, 128, (51,)), (19, -384, 128, (52,)), (19, -512, 128, (52,)),
)
STEPS = (
    ("J", 0, ()), ("J", 2, ()), ("J", 3, ()), ("J", 1, ()), ("J", 8, ()), ("J", 7, ()), ("J", 6, ()), ("J", 5, ()),
    ("J", 12, ()), ("J", 11, ()), ("J", 10, ()), ("J", 13, ()), ("J", 16, ()), ("J", 15, ()), ("J", 17, ()), ("J", 18, ()),
    ("J", 20, ()), ("J", 21, ()), ("J", 22, ()), ("J", 23, ()), ("J", 25, ()), ("J", 26, ()), ("J", 27, ()), ("J", 28, ()),
    ("J", 30, ()), ("J", 31, ()), ("J", 32, ()), ("J", 33, (1,)), ("J", 35, ()), ("J", 36, ()), ("J", 37, (2,)), ("J", 4, ()),
    ("J", 39, ()), ("J", 40, ()), ("J", 9, ()), ("S", (0, 2, 512)), ("F", (3,)), ("J", 14, ()), ("S", (2, 2, 512)), ("F", ()),
    ("J", 19, ()), ("S", (4, 2, 512)), ("F", (4,)), ("J", 24, ()), ("S", (6, 2, 512)), ("F", ()), ("J", 29, ()), ("S", (0, 2, 0)),
    ("F", ()), ("J", 34, ()), ("S", (2, 2, 0)), ("F", ()), ("J", 38, ()), ("S", (4, 2, 0)), ("F", ()), ("J", 41, ()),
    ("S", (6, 2, 0)), ("F", ()), ("J", 43, ()), ("J", 42, ()), ("F", ()), ("J", 44, ()), ("F", ()), ("J", 56, ()),
    ("J", 55, ()), ("J", 62, (5,)), ("J", 45, ()), ("J", 61, ()), ("J", 68, ()), ("J", 57, ()), ("J", 67, ()), ("J", 74, ()),
    ("J", 58, ()), ("J", 73, ()), ("J", 80, ()), ("J", 46, ()), ("J", 79, ()), ("J", 86, ()), ("J", 59, ()), ("J", 85, ()),
    ("J", 63, ()), ("J", 64, ()), ("J", 91, ()), ("J", 92, ()), ("J", 69, ()), ("J", 70, (6,)), ("J", 60, ()), ("J", 47, ()),
    ("J", 75, ()), ("J", 76, ()), ("J", 66, ()), ("J", 65, ()), ("J", 81, (7,)), ("J", 82, ()), ("J", 71, ()), ("J", 72, ()),
    ("J", 88, ()), ("J", 87, ()), ("J", 78, ()), ("J", 77, ()), ("J", 94, ()), ("J", 93, ()), ("J", 83, ()), ("J", 84, ()),
    ("J", 48, ()), ("J", 89, ()), ("J", 90, ()), ("J", 51, ()), ("J", 95, ()), ("J", 96, (8,)), ("F", ()), ("J", 49, (9,)),
    ("J", 50, ()), ("J", 52, ()), ("J", 53, ()), ("S", (8, 2, 512)), ("F", (10, 11)), ("J", 54, ()), ("J", 97, ()), ("J", 98, ()),
    ("S", (10, 2, 512)), ("S", (12, 2, 512)), ("S", (14, 2, 512)), ("S", (16, 2, 512)), ("S", (18, 1, 512)), ("S", (8, 2, 0)), ("S", (10, 2, 0)), ("S", (12, 2, 0)),
    ("S", (14, 2, 0)), ("S", (16, 2, 0)), ("S", (18, 1, 0)), ("F", ()), ("J", 99, ()), ("F", ()), ("J", 100, ()), ("F", ()),
    ("J", 101, ()),
)


def plan():
    jobs = [Job(*j) for j in JOBS]
    halos = [Halo(h[0], h[1], h[2], n, h[3]) for n, h in enumerate(HALOS)]
    return jobs, halos, STEPS


HEAD_ROWS = 256
WEIGHT_WAITS = (0, 1, 3, 7, 20)


def dot(a, b):
    return jnp.dot(a, b, preferred_element_type=F32)


def stack_kernel(jobs, halos, steps, devices, x, wp, wn, b, wr, ws, S, h_out,
                 H, XH, G, W, WR, WS, B, wsem, send_sem, recv_sem):
    me = lax.axis_index("sp")
    first = me == 0

    load_x = pltpu.make_async_copy(x, H.at[0, HALO:HALO + ROWS], wsem.at[LAYERS + 1])
    load_b = pltpu.make_async_copy(b, B, wsem.at[LAYERS])
    layer_loads = []
    for layer in range(LAYERS):
        layer_loads.append([pltpu.make_async_copy(wp.at[layer], W.at[layer, 0:CH], wsem.at[layer]),
                            pltpu.make_async_copy(wn.at[layer], W.at[layer, CH:2 * CH], wsem.at[layer]),
                            pltpu.make_async_copy(wr.at[layer], WR.at[layer], wsem.at[layer])])
    load_skip = pltpu.make_async_copy(ws, WS, wsem.at[LAYERS + 2])
    for c in [load_x] + layer_loads[0] + [load_b]:
        c.start()
    for group in layer_loads[1:]:
        for c in group:
            c.start()
    load_skip.start()

    @pl.when(first)
    def _():
        XH[...] = jnp.zeros_like(XH)
        for h in halos:
            if h.layer:
                H[h.layer, HALO + h.start:HALO + h.start + h.rows] = jnp.zeros((h.rows, CH), BF16)

    barrier = pltpu.get_barrier_semaphore()

    @pl.when(me > 0)
    def _():
        pl.semaphore_signal(barrier, inc=1, device_id={"sp": me - 1}, device_id_type=pl.DeviceIdType.MESH)

    @pl.when(me < devices - 1)
    def _():
        pl.semaphore_wait(barrier, 1)

    def remote(h):
        src = H.at[h.layer, HALO + ROWS + h.start:HALO + ROWS + h.start + h.rows]
        dst = H.at[h.layer, HALO + h.start:HALO + h.start + h.rows] if h.layer else XH.at[XROWS + h.start:XROWS + h.start + h.rows]
        return pltpu.make_async_remote_copy(
            src_ref=src, dst_ref=dst, send_sem=send_sem.at[h.index], recv_sem=recv_sem.at[h.index],
            device_id={"sp": lax.rem(me + 1, devices)}, device_id_type=pl.DeviceIdType.MESH)

    finished, gated, arrived, weighed, summed = set(), set(), set(), set(), set()

    def wait_for(n):
        layer, skip_too = jobs[n].layer, "skip" not in weighed
        if layer not in weighed:
            low = max(k for k in WEIGHT_WAITS if k <= layer)
            high = min(k for k in WEIGHT_WAITS if k > layer)
            for k in range(low, high):
                weighed.add(k)
                for c in layer_loads[k]:
                    c.wait()
            if high == LAYERS and skip_too:
                weighed.add("skip")
                load_skip.wait()
        for h in jobs[n].halos:
            if h not in arrived:
                arrived.add(h)
                pl.when(me > 0)(remote(halos[h]).wait_recv)
                if not halos[h].layer:
                    H[0, HALO - XROWS:HALO] = XH[...]

    def send(which):
        for h in which:
            assert finished.issuperset(halos[h].needs)
            pl.when(me < devices - 1)(remote(halos[h]).start)

    def z_stage(job):
        at, d = HALO + job.start, dil(job.layer)
        both = jnp.concatenate([H[job.layer, at - d:at - d + job.rows], H[job.layer, at:at + job.rows]], axis=1)
        return dot(both, W[job.layer])

    def gate_stage(job, z):
        z = z + B[job.layer % CYCLE, job.layer // CYCLE:job.layer // CYCLE + 1]
        t = jnp.tanh(z[:, :CH])
        u = jnp.tanh(0.5 * z[:, CH:])
        g = (0.5 * (t * u + t)).astype(BF16)
        cut = max(-job.start, 0)
        if cut < job.rows and job.layer < LAYERS - 1:
            G[job.start + cut:job.end, job.layer * CH:(job.layer + 1) * CH] = g[cut:]
        return g

    def fin_stage(n, g):
        job = jobs[n]
        at = HALO + job.start
        new = (H[job.layer, at:at + job.rows].astype(F32) + dot(g, WR[job.layer])).astype(BF16)
        if job.layer == LAYERS - 1:
            h_out[job.start:job.end] = new
            add_skip(slice(job.start, job.end), dot(g, WS[(LAYERS - 1) * CH:]))
        elif job.start < 0:
            cut = min(-job.start, job.rows)
            H[job.layer + 1, at:at + cut] = jnp.where(first, jnp.zeros((cut, CH), BF16), new[:cut])
            if cut < job.rows:
                H[job.layer + 1, at + cut:at + job.rows] = new[cut:]
        else:
            H[job.layer + 1, at:at + job.rows] = new
        finished.add(n)

    def add_skip(rows, part):
        S[rows] = S[rows] + part if rows.start // TILE in summed else part

    def skip_stage(layer, count, start):
        for low in (start, start + TILE):
            rows = slice(low, low + TILE)
            add_skip(rows, dot(G[rows, layer * CH:(layer + count) * CH], WS[layer * CH:(layer + count) * CH]))
            summed.add(low // TILE)

    pipe = []

    def retire():
        n, g = pipe.pop()
        fin_stage(n, g)

    load_x.wait()
    send([n for n, h in enumerate(halos) if not h.layer])
    load_b.wait()
    for at, step in enumerate(steps):
        if step[0] == "S":
            assert "skip" in weighed
            skip_stage(*step[1])
            continue
        if step[0] == "J":
            n = step[1]
            assert finished.issuperset(jobs[n].needs), jobs[n]
            wait_for(n)
            g = gate_stage(jobs[n], z_stage(jobs[n]))
            gated.add(n)
        if step[-1]:
            send(step[-1])
            coming = [k[1] for k in steps[at + 1:at + 2] if k[0] == "J"]
            for k in coming:
                if not set(jobs[k].halos) & set(step[-1]):
                    wait_for(k)
        if pipe:
            retire()
        if step[0] == "J":
            pipe.append((n, g))
    if pipe:
        retire()

    @pl.when(me < devices - 1)
    def _():
        for h in halos:
            remote(h).wait_send()


def head_kernel(S, h, w1, b1, w2, b2, y, h_out, Y, sem):
    pass_h = pltpu.make_async_copy(h, h_out, sem.at[0])
    pass_h.start()
    writes = []
    for n, start in enumerate(range(0, ROWS, HEAD_ROWS)):
        rows = slice(start, start + HEAD_ROWS)
        a = jnp.maximum(S[rows], 0.0).astype(BF16)
        m = jnp.maximum(dot(a, w1[...]) + b1[...], 0.0).astype(BF16)
        Y[rows] = dot(m, w2[...]) + b2[...]
        c = pltpu.make_async_copy(Y.at[rows], y.at[rows], sem.at[1 + n])
        c.start()
        writes.append(c)
    pass_h.wait()
    for c in writes:
        c.wait()


def solution(mesh):
    devices = mesh.shape["sp"]
    jobs, halos, steps = plan()
    rows = P(("ens", "sp"), None)

    def local(x, wp, wn, b, wr, ws, w1, b1, w2, b2):
        hbm, near = pl.BlockSpec(memory_space=pltpu.HBM), pl.BlockSpec(memory_space=pltpu.VMEM)
        vmem = lambda *shape: pltpu.VMEM(shape, BF16)
        skip, hidden = pl.pallas_call(
            lambda *refs: stack_kernel(jobs, halos, steps, devices, *refs),
            out_shape=(pltpu.VMEM((ROWS, CH), F32), pltpu.VMEM((ROWS, CH), BF16)),
            in_specs=[hbm] * 6,
            out_specs=(near, near),
            scratch_shapes=[
                vmem(LAYERS, HALO + ROWS, CH), vmem(XROWS, CH), vmem(ROWS, (LAYERS - 1) * CH),
                vmem(LAYERS, 2 * CH, 2 * CH), vmem(LAYERS, CH, CH), vmem(LAYERS * CH, CH),
                pltpu.VMEM((CYCLE, LAYERS // CYCLE, 2 * CH), F32),
                pltpu.SemaphoreType.DMA((LAYERS + 3,)),
                pltpu.SemaphoreType.DMA((len(halos),)), pltpu.SemaphoreType.DMA((len(halos),)),
            ],
            compiler_params=pltpu.CompilerParams(collective_id=0, has_side_effects=True, vmem_limit_bytes=56 * 1024 * 1024),
            name="wavenet_stack",
        )(x, wp.reshape(LAYERS, CH, 2 * CH), wn.reshape(LAYERS, CH, 2 * CH), jnp.swapaxes(b, 0, 1),
          wr.reshape(LAYERS, CH, CH), ws.reshape(LAYERS * CH, CH))
        return pl.pallas_call(
            head_kernel,
            out_shape=(jax.ShapeDtypeStruct((ROWS, CH), F32), jax.ShapeDtypeStruct((ROWS, CH), BF16)),
            in_specs=[near] * 6,
            out_specs=(hbm, hbm),
            scratch_shapes=[pltpu.VMEM((ROWS, CH), F32), pltpu.SemaphoreType.DMA((1 + ROWS // HEAD_ROWS,))],
            compiler_params=pltpu.CompilerParams(vmem_limit_bytes=6 * 1024 * 1024),
            name="wavenet_head",
        )(skip, hidden, w1, b1.reshape(1, CH), w2, b2.reshape(1, CH))

    return jax.shard_map(local, mesh=mesh, in_specs=(rows,) + (P(),) * 9, out_specs=(rows, rows), check_vma=False)
```

time: 166 us -> 29.8 us (0.18)
  waiting for transfers between devices: 79.7 us -> 0 us
  starting transfers between devices: 39 us -> 0 us
  matrix products: 34.6 us -> 0 us
  Pallas kernels: 0 us -> 28.3 us
  other arithmetic: 8.32 us -> 0 us
    ppermute x20 -> x0, waiting for transfers between devices: 79.7 us -> none  [local_stack(): halo_rows = lax.ppermute(hidden[-dilation:], 'sp', perm=shift_perm)]
    ppermute x20 -> x0, starting transfers between devices: 39 us -> none  [local_stack(): halo_rows = lax.ppermute(hidden[-dilation:], 'sp', perm=shift_perm)]
    dot_general x81 -> x0, matrix products: 34.6 us -> none  [the longest x20 9.8 us: local_stack(): jnp.dot(hidden, w_now[stack_idx, layer_pos], preferred_element_type=jnp.f...]
    pallas_call x0 -> x2, Pallas kernels: none -> 28.3 us  [the longest x1 27 us: local(): pl.pallas_call(lambda *refs: stack_kernel(jobs, halos, steps, devices, *r...]
    convert_element_type x20 -> x0, other arithmetic: 8.32 us -> none  [local_stack(): (jnp.tanh(pre_act[:, :gate_ch]) * jax.nn.sigmoid(pre_act[:, gate_ch:])).a...]
  transfers between devices with their start and end apart: 20 -> 0, of which waited for: 20 -> 0; matrix products, arithmetic and copies ran while one was open for 5% -> 0% of each run, Pallas kernels for 0% -> 0%
where the time goes in v3:
time: 29.8 us; the launch traced here: 29.2 us
  Pallas kernels  28.3 us (95%)
  between operations  0.87 us (3%)
    pallas_call x1, Pallas kernels, local(): pl.pallas_call(lambda *refs: stack_kernel(jobs, halos, steps, devices, *r...  27 us
    pallas_call x1, Pallas kernels, local(): pl.pallas_call(head_kernel, out_shape=(jax.ShapeDtypeStruct((ROWS, CH), F...  1.35 us

profile of v3, /device:TPU:4, one launch (start us, length us, event | category | flops | bytes accessed | tf_op | source)
XLA Modules:
  0.0 29.2 jit_solution(7873252317953792044)
XLA Ops:
  0.6 0.0 copy-start
  0.6 0.0 copy-start.1
  0.7 0.0 copy-start.2
  0.7 0.0 copy-start.3
  0.7 27.0 %wavenet_stack.1 = (f32[1024,256]{1,0:T(8,128)S(1)}, bf16[1024,256]{1,0:T(8,128)(2,1)S(1)}) custom-call(bf16[1024,256]{1,0:T(8,128)(2,1)} %refs_0_.1, bf16[20,256,512]{2,1,0:T(8,128)(2,1)} %bitcast.9, bf16[20,256,512]{2,1,0:T(8,128)(2,1)} %bitcast.10, f32[10,2,512]{2,1,0:T(2,128)} %bitcast.13, bf16[20,256,256]{2,1,0:T(8,128)(2,1)} %bitcast.11, ...), custom_call_target="tpu_custom_call" | custom-call | tf_op jit(solution)/shard_map/wavenet_stack/pallas_call | solution.py:295
  27.7 0.0 copy-done
  27.7 0.0 copy-done.1
  27.7 0.0 copy-done.2
  27.7 0.0 copy-done.3
  27.7 1.3 %wavenet_head.1 = (f32[1024,256]{1,0:T(8,128)}, bf16[1024,256]{1,0:T(8,128)(2,1)}) custom-call(f32[1024,256]{1,0:T(8,128)S(1)} %get-tuple-element.4.S, bf16[1024,256]{1,0:T(8,128)(2,1)S(1)} %get-tuple-element.5.h, bf16[256,256]{1,0:T(8,128)(2,1)S(1)} %copy-done, f32[1,256]{1,0:T(1,128)S(1)} %bitcast.7, bf16[256,256]{1,0:T(8,128)(2,1)S(1)} %copy-done.1, ...), custom_call_target="tpu_custom_call" | custom-call | tf_op jit(solution)/shard_map/wavenet_head/pallas_call | solution.py:311
Async XLA Ops:
  0.6 27.0 %copy-start = (bf16[256,256]{1,0:T(8,128)(2,1)S(1)}, bf16[256,256]{1,0:T(8,128)(2,1)}, u32[]{:S(2)}) copy-start(bf16[256,256]{1,0:T(8,128)(2,1)} %w1.1) | copy-start | bytes 393220
  0.6 27.0 %copy-start.1 = (bf16[256,256]{1,0:T(8,128)(2,1)S(1)}, bf16[256,256]{1,0:T(8,128)(2,1)}, u32[]{:S(2)}) copy-start(bf16[256,256]{1,0:T(8,128)(2,1)} %w2.1) | copy-start | bytes 393220
  0.7 27.0 %copy-start.2 = (f32[256]{0:T(256)S(1)}, f32[256]{0:T(256)}, u32[]{:S(2)}) copy-start(f32[256]{0:T(256)} %param.17) | copy-start | bytes 3076
  0.7 27.0 %copy-start.3 = (f32[256]{0:T(256)S(1)}, f32[256]{0:T(256)}, u32[]{:S(2)}) copy-start(f32[256]{0:T(256)} %param.19) | copy-start | bytes 3076

commit v4 on v3

v4 whole, which is shorter than its diff:
```python
import dataclasses

import jax
import jax.numpy as jnp
from jax import lax
from jax.experimental import pallas as pl
from jax.experimental.pallas import tpu as pltpu
from jax.sharding import PartitionSpec as P

F32, BF16 = jnp.float32, jnp.bfloat16
ROWS, CH, LAYERS, CYCLE = 1024, 256, 20, 10
HALO = 256
XROWS = 128
TILE = 256
CUTS = (512, 256)
GROUPS = ()

FIRST_SKIP, FLUSH, FIRST_SEND, END = 128, 159, 160, 255
ORDER = (
    0xc0b0a0807060503010002, 0x1a19171615141211100f0d, 0xa209212304a1201f1e1c1b, 0x9f80189fa31328270e2524,
    0x299fa4269f8382229f811d, 0x389f2c9f8d2a8c8b2b9f8a, 0x3f404a393a443d2da53e37, 0x554b564f4650493b45432e,
    0x52a7a651412f424c5b3c5c, 0x3054535e5d4d4e58574847, 0x3432a9319fa8605f335a59, 0x629f86368561abaa9f8435,
    0x9f93639291908f8e898887, 0xffffffffffffffff659f64,
)


def dil(layer):
    return 2 ** (layer % CYCLE)


@dataclasses.dataclass
class Job:
    layer: int
    start: int
    rows: int
    valid: int
    needs: list = dataclasses.field(default_factory=list)
    halos: list = dataclasses.field(default_factory=list)

    @property
    def end(self):
        return self.start + self.rows


@dataclasses.dataclass
class Halo:
    layer: int
    start: int
    rows: int
    index: int
    needs: list = dataclasses.field(default_factory=list)


def make_jobs():
    jobs = []

    def add(layer, start, rows, valid=None):
        jobs.append(Job(layer, start, rows, start if valid is None else valid))

    for layer in range(7):
        reach = 2 * dil(layer)
        for start in (768, 512, 256):
            add(layer, start, TILE)
        if layer < 6:
            add(layer, 0, TILE, reach - 1)
        else:
            add(layer, 64, TILE - 64, reach - 1)
        low, high = (-128, 64) if layer < 5 else (-64, 64) if layer == 5 else (0, 128)
        add(layer, low, high - low, reach - XROWS)
    for layer in (7, 8, 9, 17, 18):
        for start in (768, 512, 256, 0):
            add(layer, start, TILE)
    for layer in range(10, 17):
        reach, top = 2 * dil(layer), ROWS
        for cut in CUTS + (None,):
            if cut is not None:
                low, valid = cut + 64 * (layer == 16), cut + reach - 1
            elif GROUPS:
                low, valid = 0, 0
            else:
                low, valid = max(-128, min(64 * (layer - 16), 0)) if layer > 14 else -128, reach - XROWS
            count = -(-(top - low) // TILE)
            for left in range(count, 0, -1):
                rows = -(-(top - low) // left // 64) * 64
                top -= rows
                add(layer, top, rows, max(valid, top) if left == 1 else None)
            if cut is not None:
                top = cut + (64 if layer < 16 else 128)
    for start, rows in ((768, 256), (512, 256), (256, 256), (128, 128), (0, 128)):
        add(LAYERS - 1, start, rows)
    return jobs


def make_halos():
    sizes = [(0, 128, 128), (7, 128, 128), (8, 256, 256), (9, 512, 256)]
    if GROUPS:
        sizes += [(layer, max(16, dil(layer)), max(16, dil(layer))) for layer in range(10, 17)]
    else:
        sizes += [(10, 128, 128)]
    sizes += [(17, 128, 128), (18, 256, 256), (19, 512, 128)]
    tops = [(layer, top, chunk) for layer, rows, chunk in sizes for top in range(0, rows, chunk)]
    return [Halo(layer, -top - chunk, chunk, index) for index, (layer, top, chunk) in enumerate(tops)]


def plan():
    jobs, halos = make_jobs(), make_halos()
    sent = {h.layer for h in halos}

    def cover(layer, low, high):
        found, want = [], set(range(low, high)) if layer else set()
        for n, j in enumerate(jobs):
            have = want & set(range(max(j.valid, j.start), j.end)) if j.layer == layer - 1 else set()
            if have:
                found.append(n)
                want -= have
        assert not want, (layer, low, high)
        return found

    for n, j in enumerate(jobs):
        for back in (0, dil(j.layer)):
            low, high = j.valid - back, j.end - back
            inner = low
            if low < 0 and j.layer in sent:
                inner = 0
                j.halos += [h.index for h in halos if h.layer == j.layer and h.start < high and h.start + h.rows > low and h.index not in j.halos]
            j.needs += [k for k in cover(j.layer, inner, high) if k not in j.needs]
        j.needs += [k for k, q in enumerate(jobs) if q.layer == j.layer and k != n and k not in j.needs
                    and q.start < j.end and q.valid > max(j.start, q.start, j.valid)]
    for h in halos:
        h.needs = cover(h.layer, ROWS + h.start, ROWS + h.start + h.rows)
    for group in GROUPS:
        union = sorted({k for h in halos if h.layer in group for k in h.needs})
        for h in halos:
            if h.layer in group:
                h.needs = union

    pieces = [(layer, min(2, LAYERS - 1 - layer), start) for start in (512, 0) for layer in range(0, LAYERS - 1, 2)]
    steps = []
    for code in [word >> 8 * k & 255 for word in ORDER for k in range(11)]:
        if code >= FIRST_SEND and code != END:
            steps[-1][-1].append(code - FIRST_SEND)
        elif code == FLUSH:
            steps.append(("F", []))
        elif FIRST_SKIP <= code < FLUSH:
            steps.append(("S", pieces[code - FIRST_SKIP]))
        elif code < FIRST_SKIP:
            steps.append(("J", code, []))
    return jobs, halos, steps


HEAD_ROWS = 256
WEIGHT_WAITS = (0, 1, 4, 9, 20)


def dot(a, b):
    return jnp.dot(a, b, preferred_element_type=F32)


def stack_kernel(jobs, halos, steps, devices, x, wp, wn, b, wr, ws, S, h_out,
                 H, G, W, WR, WS, B, wsem, send_sem, recv_sem, *lands):
    me = lax.axis_index("sp")
    first = me == 0
    land = dict(zip(dict.fromkeys(h.layer for h in halos), lands))

    load_x = pltpu.make_async_copy(x, H.at[0, HALO:HALO + ROWS], wsem.at[LAYERS + 1])
    load_b = pltpu.make_async_copy(b, B, wsem.at[LAYERS])
    layer_loads = []
    for layer in range(LAYERS):
        layer_loads.append([pltpu.make_async_copy(wp.at[layer], W.at[layer, 0:CH], wsem.at[layer]),
                            pltpu.make_async_copy(wn.at[layer], W.at[layer, CH:2 * CH], wsem.at[layer]),
                            pltpu.make_async_copy(wr.at[layer], WR.at[layer], wsem.at[layer])])
    load_skip = pltpu.make_async_copy(ws, WS, wsem.at[LAYERS + 2])
    for c in [load_x] + layer_loads[0] + [load_b]:
        c.start()
    for group in layer_loads[1:]:
        for c in group:
            c.start()
    load_skip.start()

    @pl.when(first)
    def _():
        for ref in lands:
            ref[...] = jnp.zeros_like(ref)

    barrier = pltpu.get_barrier_semaphore()

    @pl.when(me > 0)
    def _():
        pl.semaphore_signal(barrier, inc=1, device_id={"sp": me - 1}, device_id_type=pl.DeviceIdType.MESH)

    @pl.when(me < devices - 1)
    def _():
        pl.semaphore_wait(barrier, 1)

    def remote(h):
        src = H.at[h.layer, HALO + ROWS + h.start:HALO + ROWS + h.start + h.rows]
        at = land[h.layer].shape[0] + h.start
        dst = land[h.layer].at[at:at + h.rows]
        return pltpu.make_async_remote_copy(
            src_ref=src, dst_ref=dst, send_sem=send_sem.at[h.index], recv_sem=recv_sem.at[h.index],
            device_id={"sp": lax.rem(me + 1, devices)}, device_id_type=pl.DeviceIdType.MESH)

    finished, gated, arrived, weighed, summed = set(), set(), set(), set(), set()

    def wait_weights(layer):
        if layer not in weighed:
            low = max(k for k in WEIGHT_WAITS if k <= layer)
            high = min(k for k in WEIGHT_WAITS if k > layer)
            for k in range(low, high):
                weighed.add(k)
                for c in layer_loads[k]:
                    c.wait()
            if high == LAYERS:
                weighed.add("skip")
                load_skip.wait()

    def wait_for(n):
        wait_weights(jobs[n].layer)
        wait_halos(n)

    def wait_halos(n):
        if jobs[n].halos:
            wait_weights(LAYERS - 1)
        for h in jobs[n].halos:
            if h not in arrived:
                arrived.add(h)
                pl.when(me > 0)(remote(halos[h]).wait_recv)
                if halos[h].layer % CYCLE == 0:
                    H[halos[h].layer, HALO - XROWS:HALO] = land[halos[h].layer][...]

    def send(which):
        for h in which:
            assert finished.issuperset(halos[h].needs)
            pl.when(me < devices - 1)(remote(halos[h]).start)

    def z_stage(job):
        low, high, d = job.start, job.end, dil(job.layer)
        now = H[job.layer, HALO + low:HALO + high]
        if job.halos and job.layer % CYCLE:
            past = land[job.layer][low:min(high, d)]
            if high > d:
                past = jnp.concatenate([past, H[job.layer, HALO:HALO + high - d]], axis=0)
        else:
            past = H[job.layer, HALO + low - d:HALO + high - d]
        return dot(jnp.concatenate([past, now], axis=1), W[job.layer])

    def gate_stage(job, z):
        z = z + B[job.layer % CYCLE, job.layer // CYCLE:job.layer // CYCLE + 1]
        t = jnp.tanh(z[:, :CH])
        u = jnp.tanh(0.5 * z[:, CH:])
        g = (0.5 * (t * u + t)).astype(BF16)
        cut = max(-job.start, 0)
        if cut < job.rows and job.layer < LAYERS - 1:
            G[job.start + cut:job.end, job.layer * CH:(job.layer + 1) * CH] = g[cut:]
        return g

    def fin_stage(n, g):
        job = jobs[n]
        at = HALO + job.start
        new = (H[job.layer, at:at + job.rows].astype(F32) + dot(g, WR[job.layer])).astype(BF16)
        if job.layer == LAYERS - 1:
            h_out[job.start:job.end] = new
            add_skip(slice(job.start, job.end), dot(g, WS[(LAYERS - 1) * CH:]))
        elif job.start < 0:
            cut = min(-job.start, job.rows)
            H[job.layer + 1, at:at + cut] = jnp.where(first, jnp.zeros((cut, CH), BF16), new[:cut])
            if cut < job.rows:
                H[job.layer + 1, at + cut:at + job.rows] = new[cut:]
        else:
            H[job.layer + 1, at:at + job.rows] = new
        finished.add(n)

    def add_skip(rows, part):
        S[rows] = S[rows] + part if rows.start // TILE in summed else part

    def skip_stage(layer, count, start):
        for low in (start, start + TILE):
            rows = slice(low, low + TILE)
            add_skip(rows, dot(G[rows, layer * CH:(layer + count) * CH], WS[layer * CH:(layer + count) * CH]))
            summed.add(low // TILE)

    pipe = []

    def retire():
        n, g = pipe.pop()
        fin_stage(n, g)

    load_x.wait()
    send([n for n, h in enumerate(halos) if not h.layer])
    load_b.wait()
    for at, step in enumerate(steps):
        if step[0] == "S":
            assert "skip" in weighed
            skip_stage(*step[1])
            continue
        if step[0] == "J":
            n = step[1]
            assert finished.issuperset(jobs[n].needs), jobs[n]
            wait_for(n)
            g = gate_stage(jobs[n], z_stage(jobs[n]))
            gated.add(n)
        if pipe:
            retire()
        if step[-1]:
            send(step[-1])
            for k in [k[1] for k in steps[at + 1:at + 2] if k[0] == "J"]:
                wait_for(k)
        if step[0] == "J":
            pipe.append((n, g))
    if pipe:
        retire()

    @pl.when(me < devices - 1)
    def _():
        for h in halos:
            remote(h).wait_send()


def head_kernel(S, h, w1, b1, w2, b2, y, h_out, Y, sem):
    pass_h = pltpu.make_async_copy(h, h_out, sem.at[0])
    pass_h.start()
    writes = []
    for n, start in enumerate(range(0, ROWS, HEAD_ROWS)):
        rows = slice(start, start + HEAD_ROWS)
        a = jnp.maximum(S[rows], 0.0).astype(BF16)
        m = jnp.maximum(dot(a, w1[...]) + b1[...], 0.0).astype(BF16)
        Y[rows] = dot(m, w2[...]) + b2[...]
        c = pltpu.make_async_copy(Y.at[rows], y.at[rows], sem.at[1 + n])
        c.start()
        writes.append(c)
    pass_h.wait()
    for c in writes:
        c.wait()


def solution(mesh):
    devices = mesh.shape["sp"]
    jobs, halos, steps = plan()
    tall = {h.layer: max(-k.start for k in halos if k.layer == h.layer) for h in halos}
    rows = P(("ens", "sp"), None)

    def local(x, wp, wn, b, wr, ws, w1, b1, w2, b2):
        hbm, near = pl.BlockSpec(memory_space=pltpu.HBM), pl.BlockSpec(memory_space=pltpu.VMEM)
        vmem = lambda *shape: pltpu.VMEM(shape, BF16)
        skip, hidden = pl.pallas_call(
            lambda *refs: stack_kernel(jobs, halos, steps, devices, *refs),
            out_shape=(pltpu.VMEM((ROWS, CH), F32), pltpu.VMEM((ROWS, CH), BF16)),
            in_specs=[hbm] * 6,
            out_specs=(near, near),
            scratch_shapes=[
                vmem(LAYERS, HALO + ROWS, CH), vmem(ROWS, (LAYERS - 1) * CH),
                vmem(LAYERS, 2 * CH, 2 * CH), vmem(LAYERS, CH, CH), vmem(LAYERS * CH, CH),
                pltpu.VMEM((CYCLE, LAYERS // CYCLE, 2 * CH), F32),
                pltpu.SemaphoreType.DMA((LAYERS + 3,)),
                pltpu.SemaphoreType.DMA((len(halos),)), pltpu.SemaphoreType.DMA((len(halos),)),
            ] + [vmem(n, CH) for n in tall.values()],
            compiler_params=pltpu.CompilerParams(collective_id=0, has_side_effects=True, vmem_limit_bytes=56 * 1024 * 1024),
            name="wavenet_stack",
        )(x, wp.reshape(LAYERS, CH, 2 * CH), wn.reshape(LAYERS, CH, 2 * CH), jnp.swapaxes(b, 0, 1),
          wr.reshape(LAYERS, CH, CH), ws.reshape(LAYERS * CH, CH))
        return pl.pallas_call(
            head_kernel,
            out_shape=(jax.ShapeDtypeStruct((ROWS, CH), F32), jax.ShapeDtypeStruct((ROWS, CH), BF16)),
            in_specs=[near] * 6,
            out_specs=(hbm, hbm),
            scratch_shapes=[pltpu.VMEM((ROWS, CH), F32), pltpu.SemaphoreType.DMA((1 + ROWS // HEAD_ROWS,))],
            compiler_params=pltpu.CompilerParams(vmem_limit_bytes=6 * 1024 * 1024),
            name="wavenet_head",
        )(skip, hidden, w1, b1.reshape(1, CH), w2, b2.reshape(1, CH))

    return jax.shard_map(local, mesh=mesh, in_specs=(rows,) + (P(),) * 9, out_specs=(rows, rows), check_vma=False)
```

time: 29.8 us -> 29.3 us (0.983); the launches traced: 29.2 us -> 29.1 us
  no operation moved by 1% of the time
where the time goes in v4:
time: 29.3 us; the launch traced here: 29.1 us
  Pallas kernels  28.2 us (96%)
  between operations  0.87 us (3%)
    pallas_call x1, Pallas kernels, local(): pl.pallas_call(lambda *refs: stack_kernel(jobs, halos, steps, devices, *r...  26.8 us
    pallas_call x1, Pallas kernels, local(): pl.pallas_call(head_kernel, out_shape=(jax.ShapeDtypeStruct((ROWS, CH), F...  1.35 us

profile of v4, /device:TPU:4, one launch (start us, length us, event | category | flops | bytes accessed | tf_op | source)
XLA Modules:
  0.0 29.1 jit_solution(12379031217218585337)
XLA Ops:
  0.6 0.0 copy-start
  0.6 0.0 copy-start.1
  0.7 0.0 copy-start.2
  0.7 0.0 copy-start.3
  0.7 26.8 %wavenet_stack.1 = (f32[1024,256]{1,0:T(8,128)S(1)}, bf16[1024,256]{1,0:T(8,128)(2,1)S(1)}) custom-call(bf16[1024,256]{1,0:T(8,128)(2,1)} %refs_0_.1, bf16[20,256,512]{2,1,0:T(8,128)(2,1)} %bitcast.9, bf16[20,256,512]{2,1,0:T(8,128)(2,1)} %bitcast.10, f32[10,2,512]{2,1,0:T(2,128)} %bitcast.13, bf16[20,256,256]{2,1,0:T(8,128)(2,1)} %bitcast.11, ...), custom_call_target="tpu_custom_call" | custom-call | tf_op jit(solution)/shard_map/wavenet_stack/pallas_call | solution.py:345
  27.5 0.0 copy-done
  27.5 0.0 copy-done.1
  27.5 0.0 copy-done.2
  27.5 0.0 copy-done.3
  27.6 1.3 %wavenet_head.1 = (f32[1024,256]{1,0:T(8,128)}, bf16[1024,256]{1,0:T(8,128)(2,1)}) custom-call(f32[1024,256]{1,0:T(8,128)S(1)} %get-tuple-element.4.S, bf16[1024,256]{1,0:T(8,128)(2,1)S(1)} %get-tuple-element.5.h, bf16[256,256]{1,0:T(8,128)(2,1)S(1)} %copy-done, f32[1,256]{1,0:T(1,128)S(1)} %bitcast.7, bf16[256,256]{1,0:T(8,128)(2,1)S(1)} %copy-done.1, ...), custom_call_target="tpu_custom_call" | custom-call | tf_op jit(solution)/shard_map/wavenet_head/pallas_call | solution.py:361
Async XLA Ops:
  0.6 26.9 %copy-start = (bf16[256,256]{1,0:T(8,128)(2,1)S(1)}, bf16[256,256]{1,0:T(8,128)(2,1)}, u32[]{:S(2)}) copy-start(bf16[256,256]{1,0:T(8,128)(2,1)} %w1.1) | copy-start | bytes 393220
  0.6 26.9 %copy-start.1 = (bf16[256,256]{1,0:T(8,128)(2,1)S(1)}, bf16[256,256]{1,0:T(8,128)(2,1)}, u32[]{:S(2)}) copy-start(bf16[256,256]{1,0:T(8,128)(2,1)} %w2.1) | copy-start | bytes 393220
  0.7 26.9 %copy-start.2 = (f32[256]{0:T(256)S(1)}, f32[256]{0:T(256)}, u32[]{:S(2)}) copy-start(f32[256]{0:T(256)} %param.17) | copy-start | bytes 3076
  0.7 26.9 %copy-start.3 = (f32[256]{0:T(256)S(1)}, f32[256]{0:T(256)}, u32[]{:S(2)}) copy-start(f32[256]{0:T(256)} %param.19) | copy-start | bytes 3076

commit v5 on v4

--- a/solution.py
+++ b/solution.py
@@ -149,6 +149,7 @@
 
 
 HEAD_ROWS = 256
+ENTER = 1
 WEIGHT_WAITS = (0, 1, 4, 9, 20)
 
 
@@ -188,10 +189,6 @@
     def _():
         pl.semaphore_signal(barrier, inc=1, device_id={"sp": me - 1}, device_id_type=pl.DeviceIdType.MESH)
 
-    @pl.when(me < devices - 1)
-    def _():
-        pl.semaphore_wait(barrier, 1)
-
     def remote(h):
         src = H.at[h.layer, HALO + ROWS + h.start:HALO + ROWS + h.start + h.rows]
         at = land[h.layer].shape[0] + h.start
@@ -206,6 +203,8 @@
         if layer not in weighed:
             low = max(k for k in WEIGHT_WAITS if k <= layer)
             high = min(k for k in WEIGHT_WAITS if k > layer)
+            if low == ENTER:
+                enter()
             for k in range(low, high):
                 weighed.add(k)
                 for c in layer_loads[k]:
@@ -213,6 +212,12 @@
             if high == LAYERS:
                 weighed.add("skip")
                 load_skip.wait()
+
+    def enter():
+        @pl.when(me < devices - 1)
+        def _():
+            pl.semaphore_wait(barrier, 1)
+        send([n for n, h in enumerate(halos) if not h.layer])
 
     def wait_for(n):
         wait_weights(jobs[n].layer)
@@ -286,7 +291,6 @@
         fin_stage(n, g)
 
     load_x.wait()
-    send([n for n, h in enumerate(halos) if not h.layer])
     load_b.wait()
     for at, step in enumerate(steps):
         if step[0] == "S":

time: 29.3 us -> 28.5 us (0.973)
  Pallas kernels: 28.2 us -> 27.6 us
    pallas_call x1, Pallas kernels: 26.8 us -> 26.2 us  [local(): pl.pallas_call(lambda *refs: stack_kernel(jobs, halos, steps, devices, *r...]
where the time goes in v5:
time: 28.5 us; the launch traced here: 28.4 us
  Pallas kernels  27.6 us (97%)
  between operations  0.87 us (3%)
    pallas_call x1, Pallas kernels, local(): pl.pallas_call(lambda *refs: stack_kernel(jobs, halos, steps, devices, *r...  26.2 us
    pallas_call x1, Pallas kernels, local(): pl.pallas_call(head_kernel, out_shape=(jax.ShapeDtypeStruct((ROWS, CH), F...  1.35 us

profile of v5, /device:TPU:4, one launch (start us, length us, event | category | flops | bytes accessed | tf_op | source)
XLA Modules:
  0.0 28.4 jit_solution(15079279963581378295)
XLA Ops:
  0.6 0.0 copy-start
  0.6 0.0 copy-start.1
  0.7 0.0 copy-start.2
  0.7 0.0 copy-start.3
  0.7 26.2 %wavenet_stack.1 = (f32[1024,256]{1,0:T(8,128)S(1)}, bf16[1024,256]{1,0:T(8,128)(2,1)S(1)}) custom-call(bf16[1024,256]{1,0:T(8,128)(2,1)} %refs_0_.1, bf16[20,256,512]{2,1,0:T(8,128)(2,1)} %bitcast.9, bf16[20,256,512]{2,1,0:T(8,128)(2,1)} %bitcast.10, f32[10,2,512]{2,1,0:T(2,128)} %bitcast.13, bf16[20,256,256]{2,1,0:T(8,128)(2,1)} %bitcast.11, ...), custom_call_target="tpu_custom_call" | custom-call | tf_op jit(solution)/shard_map/wavenet_stack/pallas_call | solution.py:349
  26.9 0.0 copy-done
  26.9 0.0 copy-done.1
  26.9 0.0 copy-done.2
  26.9 0.0 copy-done.3
  26.9 1.3 %wavenet_head.1 = (f32[1024,256]{1,0:T(8,128)}, bf16[1024,256]{1,0:T(8,128)(2,1)}) custom-call(f32[1024,256]{1,0:T(8,128)S(1)} %get-tuple-element.4.S, bf16[1024,256]{1,0:T(8,128)(2,1)S(1)} %get-tuple-element.5.h, bf16[256,256]{1,0:T(8,128)(2,1)S(1)} %copy-done, f32[1,256]{1,0:T(1,128)S(1)} %bitcast.7, bf16[256,256]{1,0:T(8,128)(2,1)S(1)} %copy-done.1, ...), custom_call_target="tpu_custom_call" | custom-call | tf_op jit(solution)/shard_map/wavenet_head/pallas_call | solution.py:365
Async XLA Ops:
  0.6 26.3 %copy-start = (bf16[256,256]{1,0:T(8,128)(2,1)S(1)}, bf16[256,256]{1,0:T(8,128)(2,1)}, u32[]{:S(2)}) copy-start(bf16[256,256]{1,0:T(8,128)(2,1)} %w1.1) | copy-start | bytes 393220
  0.6 26.3 %copy-start.1 = (bf16[256,256]{1,0:T(8,128)(2,1)S(1)}, bf16[256,256]{1,0:T(8,128)(2,1)}, u32[]{:S(2)}) copy-start(bf16[256,256]{1,0:T(8,128)(2,1)} %w2.1) | copy-start | bytes 393220
  0.7 26.3 %copy-start.2 = (f32[256]{0:T(256)S(1)}, f32[256]{0:T(256)}, u32[]{:S(2)}) copy-start(f32[256]{0:T(256)} %param.17) | copy-start | bytes 3076
  0.7 26.3 %copy-start.3 = (f32[256]{0:T(256)S(1)}, f32[256]{0:T(256)}, u32[]{:S(2)}) copy-start(f32[256]{0:T(256)} %param.19) | copy-start | bytes 3076

commit v6 on v5

--- a/solution.py
+++ b/solution.py
@@ -17,8 +17,8 @@
 
 FIRST_SKIP, FLUSH, FIRST_SEND, END = 128, 159, 160, 255
 ORDER = (
-    0xc0b0a0807060503010002, 0x1a19171615141211100f0d, 0xa209212304a1201f1e1c1b, 0x9f80189fa31328270e2524,
-    0x299fa4269f8382229f811d, 0x389f2c9f8d2a8c8b2b9f8a, 0x3f404a393a443d2da53e37, 0x554b564f4650493b45432e,
+    0xc0b0a0807060503010002, 0x1a19171615141211100f0d, 0xa209212304a1201f1e1c1b, 0x1d9f80189f1328270e2524,
+    0x299fa4a3269f8382229f81, 0x389f2c9f8d2a8c8b2b9f8a, 0x3f404a393a443d2da53e37, 0x554b564f4650493b45432e,
     0x52a7a651412f424c5b3c5c, 0x3054535e5d4d4e58574847, 0x3432a9319fa8605f335a59, 0x629f86368561abaa9f8435,
     0x9f93639291908f8e898887, 0xffffffffffffffff659f64,
 )

time: 28.5 us -> 28.8 us (1.011)
  no operation moved by 1% of the time
where the time goes in v6:
time: 28.8 us; the launch traced here: 28.7 us
  Pallas kernels  27.8 us (97%)
  between operations  0.87 us (3%)
    pallas_call x1, Pallas kernels, local(): pl.pallas_call(lambda *refs: stack_kernel(jobs, halos, steps, devices, *r...  26.5 us
    pallas_call x1, Pallas kernels, local(): pl.pallas_call(head_kernel, out_shape=(jax.ShapeDtypeStruct((ROWS, CH), F...  1.35 us

profile of v6, /device:TPU:4, one launch (start us, length us, event | category | flops | bytes accessed | tf_op | source)
XLA Modules:
  0.0 28.7 jit_solution(6087306828221196823)
XLA Ops:
  0.6 0.0 copy-start
  0.6 0.0 copy-start.1
  0.7 0.0 copy-start.2
  0.7 0.0 copy-start.3
  0.7 26.5 %wavenet_stack.1 = (f32[1024,256]{1,0:T(8,128)S(1)}, bf16[1024,256]{1,0:T(8,128)(2,1)S(1)}) custom-call(bf16[1024,256]{1,0:T(8,128)(2,1)} %refs_0_.1, bf16[20,256,512]{2,1,0:T(8,128)(2,1)} %bitcast.9, bf16[20,256,512]{2,1,0:T(8,128)(2,1)} %bitcast.10, f32[10,2,512]{2,1,0:T(2,128)} %bitcast.13, bf16[20,256,256]{2,1,0:T(8,128)(2,1)} %bitcast.11, ...), custom_call_target="tpu_custom_call" | custom-call | tf_op jit(solution)/shard_map/wavenet_stack/pallas_call | solution.py:349
  27.1 0.0 copy-done
  27.1 0.0 copy-done.1
  27.2 0.0 copy-done.2
  27.2 0.0 copy-done.3
  27.2 1.3 %wavenet_head.1 = (f32[1024,256]{1,0:T(8,128)}, bf16[1024,256]{1,0:T(8,128)(2,1)}) custom-call(f32[1024,256]{1,0:T(8,128)S(1)} %get-tuple-element.4.S, bf16[1024,256]{1,0:T(8,128)(2,1)S(1)} %get-tuple-element.5.h, bf16[256,256]{1,0:T(8,128)(2,1)S(1)} %copy-done, f32[1,256]{1,0:T(1,128)S(1)} %bitcast.7, bf16[256,256]{1,0:T(8,128)(2,1)S(1)} %copy-done.1, ...), custom_call_target="tpu_custom_call" | custom-call | tf_op jit(solution)/shard_map/wavenet_head/pallas_call | solution.py:365
Async XLA Ops:
  0.6 26.5 %copy-start = (bf16[256,256]{1,0:T(8,128)(2,1)S(1)}, bf16[256,256]{1,0:T(8,128)(2,1)}, u32[]{:S(2)}) copy-start(bf16[256,256]{1,0:T(8,128)(2,1)} %w1.1) | copy-start | bytes 393220
  0.6 26.5 %copy-start.1 = (bf16[256,256]{1,0:T(8,128)(2,1)S(1)}, bf16[256,256]{1,0:T(8,128)(2,1)}, u32[]{:S(2)}) copy-start(bf16[256,256]{1,0:T(8,128)(2,1)} %w2.1) | copy-start | bytes 393220
  0.7 26.5 %copy-start.2 = (f32[256]{0:T(256)S(1)}, f32[256]{0:T(256)}, u32[]{:S(2)}) copy-start(f32[256]{0:T(256)} %param.17) | copy-start | bytes 3076
  0.7 26.5 %copy-start.3 = (f32[256]{0:T(256)S(1)}, f32[256]{0:T(256)}, u32[]{:S(2)}) copy-start(f32[256]{0:T(256)} %param.19) | copy-start | bytes 3076
